TPU v7x, 32 devices: a whole 2x2x4 slice. The times are simulated.
32 devices in a mesh: gx: 16 (over z, y, x), yz: 2 (over core).
Axes of the slice: x: 2, y: 2, z: 4, core: 2. Of those that a mesh axis runs over, the one named last changes fastest.
Arguments:
- magnet: bfloat16 [256, 3, 16, 256], P('yz', None, 'gx'), may hold values from -5 to 5
- newell: bfloat16 [256, 6, 16, 256], P('yz'), may hold values from -0.875 to 0.875
Outputs:
- field: bfloat16 [256, 3, 16, 256], P('yz', None, 'gx')
All inputs are finite; a program needn't handle non-finite values.
Results may differ from a plain program's by a relative error of at most 0.0055.
Values may be sent and summed in bfloat16 or wider, within the bound.
A program may use at most 256 MiB of HBM per device.

v0:
```python
import functools
import math

import jax
import jax.numpy as jnp
import ml_dtypes
import numpy as np
from jax import lax
from jax.experimental import pallas as pl
from jax.experimental.pallas import tpu as pltpu
from jax.sharding import PartitionSpec as P

EXCHANGE = 0.2
F32 = jnp.float32
BF16 = jnp.bfloat16
MESH = pl.DeviceIdType.MESH


def ky_owned(groups, parts, pairs, length):
    order = []
    for part in range(parts):
        for g in range(groups):
            first = [(g * parts + part) * pairs + p for p in range(pairs)]
            mirror = [(length - t) if t else length // 2 for t in first]
            order.append(first + mirror)
    return np.array(order).reshape(parts, -1)


def tables(groups, parts, y_total, z_total):
    pairs = y_total // (groups * parts * 2)
    rows = y_total // parts
    order = ky_owned(groups, parts, pairs, y_total)

    def trig(k, n, length):
        angle = (k[:, None] * n[None, :] % length) * (2.0 * math.pi / length)
        return np.cos(angle), np.sin(angle)

    forward, inverse = [], []
    for part in range(parts):
        own_first = (np.arange(y_total) + part * rows) % y_total
        forward.append(np.stack(trig(order[part], own_first, y_total)))
        inverse.append(np.stack(trig(own_first[:rows], order.reshape(-1), y_total)))
    half = z_total // 2
    cos, sin = trig(np.arange(z_total), np.arange(half), z_total)
    alternate = np.cos(math.pi * np.arange(z_total))
    z_fwd = np.concatenate([cos, -sin], axis=1)
    z_fwd[:, half] = alternate
    z_inv = -np.concatenate([cos, -sin], axis=1).T
    z_inv[0] = -0.5
    z_inv[half] = -0.5 * alternate
    reverse = np.zeros((z_total, half))
    for k in range(half):
        reverse[-k % z_total, k] = 1.0
    cast = lambda a: np.asarray(a, np.float32).astype(ml_dtypes.bfloat16)
    return (
        cast(np.stack(forward)),
        cast(np.stack(inverse)),
        cast(z_fwd),
        cast(z_inv),
        cast(reverse),
    )


def kernel(
    groups, pairs, magnet, newell, y_fwd, y_inv, z_fwd, z_inv, rev, out,
    mag, nwl, yf, yi, zf, zi, rv, halo, spec, send, recv, kern, source, back, fields, stack,
    lap, load_sem, nwl_sem, pair_sem, halo_sem, fwd_send, fwd_recv, bwd_send, bwd_recv,
    rel_send, rel_recv, hand,
):
    g = lax.axis_index("gx")
    c = lax.axis_index("yz")
    other = 1 - c
    own = 2 * pairs
    rows = magnet.shape[1]
    cells = groups
    half = magnet.shape[2] // 2

    plane = math.gcd(groups, 4)
    layers = groups // plane

    def target(k):
        layer, place = k // plane, lax.rem(k, plane)
        layer = jnp.where(2 * (g // plane) < layers, layers - 1 - layer, layer)
        return layer * plane + lax.rem(g + place, plane)

    barrier = pltpu.get_barrier_semaphore()

    @pl.when(c == 0)
    def _():
        pl.semaphore_signal(barrier, inc=1, device_id=(g, 1), device_id_type=MESH)

    loads = []
    for comp in range(3):
        loads.append(
            pltpu.make_async_copy(
                magnet.at[comp], mag.at[comp, pl.ds(0, rows), :], load_sem.at[comp]
            )
        )
    loads.append(pltpu.make_async_copy(z_fwd, zf, load_sem.at[3]))
    loads.append(pltpu.make_async_copy(y_fwd.at[c], yf, load_sem.at[4]))
    loads.append(pltpu.make_async_copy(rev, rv, load_sem.at[5]))
    loads.append(pltpu.make_async_copy(y_inv.at[c], yi, load_sem.at[6]))
    loads.append(pltpu.make_async_copy(z_inv, zi, load_sem.at[7]))
    for copy in loads:
        copy.start()

    def newell_row(part, p):
        t = (2 * g + part) * pairs + p
        return (1 - c) * t + c * lax.rem(rows - t, rows)

    near = [
        pltpu.make_async_copy(newell.at[newell_row(c, p)], nwl.at[c, p], nwl_sem.at[p])
        for p in range(pairs)
    ]
    for copy in near:
        copy.start()

    @pl.when(c == 1)
    def _():
        pl.semaphore_wait(barrier, 1)
        pl.semaphore_signal(hand.at[0], inc=1, device_id=(g, 0), device_id_type=MESH)

    @pl.when(c == 0)
    def _():
        pl.semaphore_wait(hand.at[0], 1)
        for r in range(1, groups):
            pl.semaphore_signal(
                barrier, inc=1, device_id=(lax.rem(g + r, groups), 0), device_id_type=MESH
            )

    for comp in range(3):
        loads[comp].wait()
    swap = []
    for comp in range(3):
        swap.append(
            pltpu.make_async_remote_copy(
                src_ref=mag.at[comp, pl.ds(0, rows), :],
                dst_ref=mag.at[comp, pl.ds(rows, rows), :],
                send_sem=pair_sem.at[0, comp],
                recv_sem=pair_sem.at[1, comp],
                device_id=(g, other),
                device_id_type=MESH,
            )
        )
    for copy in swap:
        copy.start()
    far = []
    for p in range(pairs):
        far.append(
            pltpu.make_async_remote_copy(
                src_ref=newell.at[newell_row(other, p)],
                dst_ref=nwl.at[c, p],
                send_sem=pair_sem.at[0, 3 + p],
                recv_sem=pair_sem.at[1, 3 + p],
                device_id=(g, other),
                device_id_type=MESH,
            )
        )
    for copy in far:
        copy.start()

    loads[3].wait()
    loads[4].wait()
    for comp in range(3):
        swap[comp].wait_recv()
        z_rows = jnp.dot(mag[comp], zf[...], preferred_element_type=F32).astype(BF16)
        cos_part = jnp.dot(yf[0], z_rows, preferred_element_type=F32)
        sin_part = jnp.dot(yf[1], z_rows, preferred_element_type=F32)
        low = 2 * comp * half
        spec[:, pl.ds(low, half)] = cos_part[:, :half] + sin_part[:, half:]
        spec[:, pl.ds(low + half, half)] = cos_part[:, half:] - sin_part[:, :half]
    for i in range(groups):
        send[i] = spec[pl.ds(i * own, own), :].astype(BF16)

    @pl.when(c == 0)
    def _():
        pl.semaphore_wait(barrier, groups - 1)
        pl.semaphore_signal(hand.at[1], inc=1, device_id=(g, 1), device_id_type=MESH)

    @pl.when(c == 1)
    def _():
        pl.semaphore_wait(hand.at[1], 1)

    def forward(i):
        r = lax.rem(i - g + groups, groups)
        return pltpu.make_async_remote_copy(
            src_ref=send.at[i],
            dst_ref=recv.at[g],
            send_sem=fwd_send.at[r],
            recv_sem=fwd_recv.at[r],
            device_id=(i, c),
            device_id_type=MESH,
        )

    def arrival(buffer, sems, who):
        r = lax.rem(g - who + groups, groups)
        return pltpu.make_async_remote_copy(
            src_ref=buffer.at[who],
            dst_ref=buffer.at[who],
            send_sem=fwd_send.at[r],
            recv_sem=sems.at[r],
            device_id=(who, c),
            device_id_type=MESH,
        )

    for k in range(groups):
        @pl.when(target(k) != g)
        def _():
            forward(target(k)).start()

    recv[g] = send[g]

    def halo_copy(side, comp):
        to = lax.rem(g + (1, groups - 1)[side], groups)
        return pltpu.make_async_remote_copy(
            src_ref=mag.at[comp, pl.ds(0, rows), :],
            dst_ref=halo.at[side, comp],
            send_sem=halo_sem.at[0, side, comp],
            recv_sem=halo_sem.at[1, side, comp],
            device_id=(to, c),
            device_id_type=MESH,
        )

    has_next, has_last = g < groups - 1, g > 0

    def halo_start(comps):
        @pl.when(has_next)
        def _():
            for comp in comps:
                halo_copy(0, comp).start()

        @pl.when(has_last)
        def _():
            for comp in comps:
                halo_copy(1, comp).start()

    halo_start((0, 1))

    for copy in near:
        copy.wait()
    for copy in far:
        copy.wait_recv()
    loads[5].wait()
    table_rows = 6 * cells
    even_rows = 4 * cells
    lane0 = lax.broadcasted_iota(jnp.int32, (table_rows, half), 1) == 0
    even = lax.broadcasted_iota(jnp.int32, (table_rows, half), 0) < even_rows
    sign = jnp.where(even, 1.0, -1.0).astype(F32)
    for p in range(pairs):
        first = nwl[0, p].reshape(table_rows, 2 * half)
        mirror = nwl[1, p].reshape(table_rows, 2 * half)
        rev_first = jnp.dot(first, rv[...], preferred_element_type=F32)
        rev_mirror = jnp.dot(mirror, rv[...], preferred_element_type=F32)
        lo_first, hi_first = first[:, :half].astype(F32), first[:, half:].astype(F32)
        lo_mirror, hi_mirror = mirror[:, :half].astype(F32), mirror[:, half:].astype(F32)
        if p == 0:
            alone = ((2 * g + c) * pairs == 0).astype(F32)
            paired = 1.0 - alone
            of_first = alone * rev_first + paired * rev_mirror
            of_mirror = alone * rev_mirror + paired * rev_first
        else:
            of_first, of_mirror = rev_mirror, rev_first
        k_first = lo_first + sign * of_first
        k_mirror = lo_mirror + sign * of_mirror
        middle = hi_first + sign * hi_mirror
        if p == 0:
            i_first = jnp.where(lane0, alone * (2.0 * hi_first) + paired * k_first, k_first)
            i_mirror = jnp.where(lane0, alone * (2.0 * hi_mirror) + paired * middle, k_mirror)
            k_mirror = jnp.where(lane0, alone * k_mirror + paired * middle, k_mirror)
        else:
            k_mirror = jnp.where(lane0, middle, k_mirror)
            i_first, i_mirror = k_first, k_mirror
        kern[pl.ds(p, table_rows, stride=own), :] = k_first
        kern[pl.ds(pairs + p, table_rows, stride=own), :] = k_mirror
        base = table_rows * own
        kern[pl.ds(base + p, even_rows, stride=own), :] = i_first[:even_rows]
        kern[pl.ds(base + pairs + p, even_rows, stride=own), :] = i_mirror[:even_rows]

    for comp in range(3):
        full = mag[comp].astype(F32)
        centre = full[:rows]
        total = pltpu.roll(full, 1, 0)[:rows] + pltpu.roll(full, 2 * rows - 1, 0)[:rows]
        total = total + pltpu.roll(centre, 1, 1) + pltpu.roll(centre, 2 * half - 1, 1)
        lap[comp] = total - 4.0 * centre

    lane = lax.broadcasted_iota(jnp.int32, (own, half), 1)
    slot = lax.broadcasted_iota(jnp.int32, (own, half), 0)
    first_t = (2 * g + c) * pairs + lax.rem(slot, pairs)
    packed = jnp.logical_and(lane == 0, first_t > 0)
    at_first = jnp.logical_and(packed, slot < pairs)
    at_mirror = jnp.logical_and(packed, slot >= pairs)

    def flip(v):
        return jnp.concatenate([v[pairs:], v[:pairs]], axis=0)

    def unpack(j):
        block = recv[j].astype(F32)
        for comp in range(3):
            re = block[:, 2 * comp * half : (2 * comp + 1) * half]
            im = block[:, (2 * comp + 1) * half : (2 * comp + 2) * half]
            re_f, im_f = flip(re), flip(im)
            new_re = jnp.where(at_first, 0.5 * (re + re_f), jnp.where(at_mirror, 0.5 * (im + im_f), re))
            new_im = jnp.where(at_first, 0.5 * (im - im_f), jnp.where(at_mirror, 0.5 * (re - re_f), im))
            source[j, 2 * comp] = new_re
            source[j, 2 * comp + 1] = new_im

    for k in range(groups - 1, -1, -1):
        who = target(k)

        @pl.when(who != g)
        def _():
            arrival(recv, fwd_recv, who).wait_recv()

        unpack(who)

    def k_of(entry, d):
        start = pl.multiple_of((entry * cells + d) * own, own)
        return kern[pl.ds(start, own), :]

    def backward(i):
        r = lax.rem(i - g + groups, groups)
        return pltpu.make_async_remote_copy(
            src_ref=back.at[i],
            dst_ref=fields.at[c, g],
            send_sem=bwd_send.at[r],
            recv_sem=bwd_recv.at[r],
            device_id=(i, c),
            device_id_type=MESH,
        )

    def couple(k, carry):
        i = target(k)
        acc = [jnp.zeros((own, half), F32) for _ in range(6)]
        for j in range(cells):
            d = jnp.abs(i - j)
            s = jnp.where(i >= j, 1.0, -1.0).astype(F32)
            xx, yy, zz, yz = (k_of(e, d) for e in range(4))
            xy, xz = s * k_of(4, d), s * k_of(5, d)
            xxi, yyi, zzi, yzi = (k_of(6 + e, d) for e in range(4))
            xr, xi, yr, yim, zr, zim = (source[j, q] for q in range(6))
            acc[0] += xx * xr - xy * yim - xz * zim
            acc[1] += xxi * xi + xy * yr + xz * zr
            acc[2] += yy * yr + yz * zr - xy * xi
            acc[3] += yyi * yim + yzi * zim + xy * xr
            acc[4] += yz * yr + zz * zr - xz * xi
            acc[5] += yzi * yim + zzi * zim + xz * xr
        for comp in range(3):
            re, im = acc[2 * comp], acc[2 * comp + 1]
            re_f, im_f = flip(re), flip(im)
            new_re = jnp.where(at_first, re - im_f, jnp.where(at_mirror, re_f + im, re))
            new_im = jnp.where(at_first, im + re_f, jnp.where(at_mirror, re - im_f, im))
            back[i, :, pl.ds(2 * comp * half, half)] = new_re.astype(BF16)
            back[i, :, pl.ds((2 * comp + 1) * half, half)] = new_im.astype(BF16)
        before = target(jnp.maximum(k - 1, 0))

        @pl.when(jnp.logical_and(k > 0, before != g))
        def _():
            backward(before).start()

        return carry

    lax.fori_loop(0, cells, couple, 0)

    @pl.when(target(groups - 1) != g)
    def _():
        backward(target(groups - 1)).start()

    halo_start((2,))
    fields[c, g] = back[g]

    def relay(who):
        return pltpu.make_async_remote_copy(
            src_ref=fields.at[c, who],
            dst_ref=fields.at[c, who],
            send_sem=rel_send.at[who],
            recv_sem=rel_recv.at[who],
            device_id=(g, other),
            device_id_type=MESH,
        )

    for k in range(groups - 1, -1, -1):
        who = target(k)

        @pl.when(who != g)
        def _():
            arrival(fields.at[c], bwd_recv, who).wait_recv()

        relay(who).start()
    for side, inside in enumerate((has_last, has_next)):
        @pl.when(inside)
        def _():
            for comp in range(3):
                halo_copy(side, comp).wait_recv()

        @pl.when(jnp.logical_not(inside))
        def _():
            halo[side] = mag[:, pl.ds(0, rows), :]

    for comp in range(3):
        centre = mag[comp, pl.ds(0, rows), :].astype(F32)
        x_part = halo[0, comp].astype(F32) + halo[1, comp].astype(F32) - 2.0 * centre
        lap[comp] = EXCHANGE * (lap[comp] + x_part)

    loads[6].wait()
    loads[7].wait()

    def inverse(part):
        for i in range(groups):
            stack[pl.ds(i * own, own), :] = fields[part, i].astype(F32)
        at = pl.ds(pl.multiple_of(part * rows, rows), rows)
        modes = stack[...].astype(BF16)
        return [jnp.dot(yi[t, :, at], modes, preferred_element_type=F32) for t in range(2)]

    cos_own, sin_own = inverse(c)
    for i in range(groups):
        relay(i).wait_recv()
    cos_far, sin_far = inverse(other)
    cos_all, sin_all = cos_own + cos_far, sin_own + sin_far
    scale = 1.0 / (2 * rows * 2 * half)
    for comp in range(3):
        at = slice(2 * comp * half, 2 * (comp + 1) * half)
        cos_part, sin_part = cos_all[:, at], sin_all[:, at]
        g_rows = jnp.concatenate(
            [
                cos_part[:, :half] - sin_part[:, half:],
                cos_part[:, half:] + sin_part[:, :half],
            ],
            axis=1,
        ).astype(BF16)
        demag = jnp.dot(g_rows, zi[...], preferred_element_type=F32) * scale
        out[comp] = (demag + lap[comp]).astype(BF16)

    for copy in swap + far:
        copy.wait_send()
    for i in range(groups):
        relay(i).wait_send()

        @pl.when(i != g)
        def _():
            forward(i).wait_send()
            backward(i).wait_send()

    for side, inside in enumerate((has_next, has_last)):
        @pl.when(inside)
        def _():
            for comp in range(3):
                halo_copy(side, comp).wait_send()


def on_device(magnet, newell, *consts):
    rows, _, x_cells, z_total = magnet.shape
    groups = lax.axis_size("gx")
    parts = lax.axis_size("yz")
    assert x_cells == 1 and parts == 2
    y_total = rows * parts
    pairs = y_total // (groups * parts * 2)
    own = 2 * pairs
    half = z_total // 2
    wide = 3 * z_total
    any_ref = pl.BlockSpec(memory_space=pl.ANY)
    dma = pltpu.SemaphoreType.DMA
    planes = jnp.transpose(magnet[:, :, 0, :], (1, 0, 2))
    field = pl.pallas_call(
        functools.partial(kernel, groups, pairs),
        out_shape=pltpu.VMEM(planes.shape, BF16),
        in_specs=[any_ref] * 7,
        out_specs=pl.BlockSpec(memory_space=pltpu.VMEM),
        scratch_shapes=[
            pltpu.VMEM((3, y_total, z_total), BF16),
            pltpu.VMEM((2, pairs, 6, groups, z_total), BF16),
            pltpu.VMEM((2, rows, y_total), BF16),
            pltpu.VMEM((2, rows, y_total), BF16),
            pltpu.VMEM((z_total, z_total), BF16),
            pltpu.VMEM((z_total, z_total), BF16),
            pltpu.VMEM((z_total, half), BF16),
            pltpu.VMEM((2, 3, rows, z_total), BF16),
            pltpu.VMEM((rows, wide), F32),
            pltpu.VMEM((groups, own, wide), BF16),
            pltpu.VMEM((groups, own, wide), BF16),
            pltpu.VMEM((10 * groups * own, half), F32),
            pltpu.VMEM((groups, 6, own, half), F32),
            pltpu.VMEM((groups, own, wide), BF16),
            pltpu.VMEM((2, groups, own, wide), BF16),
            pltpu.VMEM((rows, wide), F32),
            pltpu.VMEM((3, rows, z_total), F32),
            dma((8,)),
            dma((pairs,)),
            dma((2, 3 + pairs)),
            dma((2, 2, 3)),
            dma((groups,)),
            dma((groups,)),
            dma((groups,)),
            dma((groups,)),
            dma((groups,)),
            dma((groups,)),
            pltpu.SemaphoreType.REGULAR((2,)),
        ],
        compiler_params=pltpu.CompilerParams(collective_id=0, has_side_effects=True),
    )(planes, newell, *consts)
    return jnp.transpose(field, (1, 0, 2))[:, :, None, :]


def solution(mesh):
    groups, parts = mesh.shape["gx"], mesh.shape["yz"]

    def run(magnet, newell):
        consts = tables(groups, parts, magnet.shape[0], magnet.shape[3])
        body = lambda m, n: on_device(m, n, *[jnp.asarray(t) for t in consts])
        return jax.shard_map(
            body,
            mesh=mesh,
            in_specs=(P("yz", None, "gx", None), P("yz", None, None, None)),
            out_specs=P("yz", None, "gx", None),
            check_vma=False,
        )(magnet, newell)

    return run
```

profile of v0, /device:TPU:0, one launch (start us, length us, event | category | flops | bytes accessed | tf_op | source)
XLA Modules:
  0.0 24.7 jit_solution(6849054696671965430)
XLA Ops:
  0.0 24.0 %shard_map.73 = bf16[3,128,256]{2,1,0:T(8,128)(2,1)S(1)} custom-call(bf16[3,128,256]{2,1,0:T(8,128)(2,1)} %bitcast.9, bf16[128,6,16,256]{3,2,1,0:T(8,128)(2,1)} %newell.1, bf16[2,2,128,256]{3,2,1,0:T(8,128)(2,1)} %constant.10.clone.y_fwd, bf16[2,2,128,256]{3,2,1,0:T(8,128)(2,1)} %constant.11.clone.y_inv, bf16[256,256]{1,0:T(8,128)(2,1)} %constant.12.clone.z_fwd, ...), custom_call_target="tpu_custom_call" | custom-call | tf_op jit(solution)/shard_map/pallas_call | solution.py:463
  24.0 0.7 %copy.10 = bf16[128,3,1,256]{3,0,2,1:T(8,128)(2,1)} copy(bf16[128,3,1,256]{3,0,2,1:T(8,128)(2,1)S(1)} %bitcast.8) | data formatting | bytes 393216
where the time goes:
time: 24.8 us; the launch traced here: 24.7 us
  Pallas kernels  24 us (97%)
  local copies, waits for them, and re-layouts  0.68 us (3%)
    pallas_call x1, Pallas kernels, on_device(): pl.pallas_call(functools.partial(kernel, groups, pairs), out_shape=pltpu....  24 us
    unnamed x1, local copies, waits for them, and re-layouts  0.68 us

commit v1 on v0

v1 whole, which is shorter than its diff:
```python
import functools
import math

import jax
import jax.numpy as jnp
import ml_dtypes
import numpy as np
from jax import lax
from jax.experimental import pallas as pl
from jax.experimental.pallas import tpu as pltpu
from jax.sharding import PartitionSpec as P

EXCHANGE = 0.2
F32 = jnp.float32
BF16 = jnp.bfloat16
MESH = pl.DeviceIdType.MESH


def tables(couplers, parts, y_total, z_total):
    pairs = y_total // (couplers * parts * 2)
    rows = y_total // parts
    half_y = y_total // 2

    def trig(k, n, length):
        angle = (k[:, None] * n[None, :] % length) * (2.0 * math.pi / length)
        return np.cos(angle), np.sin(angle)

    def y_rows(part, n):
        blocks = []
        for m in range(couplers):
            t = (m * parts + part) * pairs + np.arange(pairs)
            cos, sin = trig(t, n, y_total)
            if t[0] == 0:
                sin[0] = trig(np.array([half_y]), n, y_total)[0][0]
            blocks += [cos, sin]
        return np.concatenate(blocks)

    half = z_total // 2
    cos, sin = trig(np.arange(z_total), np.arange(half), z_total)
    alternate = np.cos(math.pi * np.arange(z_total))
    z_fwd = np.concatenate([cos, -sin], axis=1)
    z_fwd[:, half] = alternate
    z_inv = -np.concatenate([cos, -sin], axis=1).T
    z_inv[0] = -0.5
    z_inv[half] = -0.5 * alternate
    reverse = np.zeros((z_total, half))
    for k in range(half):
        reverse[-k % z_total, k] = 1.0
    forward, inverse = [], []
    for part in range(parts):
        own_first = (np.arange(y_total) + part * rows) % y_total
        forward.append(y_rows(part, own_first))
        inverse.append(np.concatenate([y_rows(other, own_first[:rows]) for other in range(parts)]).T)
    cast = lambda a: np.asarray(a, np.float32).astype(ml_dtypes.bfloat16)
    return cast(np.stack(forward)), cast(np.stack(inverse)), cast(z_fwd), cast(z_inv), cast(reverse)


def kernel(
    groups, couplers, pairs, magnet, newell, y_fwd, y_inv, z_fwd, z_inv, rev, out,
    mag, nwl, yf, yi, zf, zi, rv, halo, zrow, spec, send, recv, kern, source, acc, back, fields, stack,
    lap, load_sem, swap_recv, pair_sem, halo_send, halo_recv, fwd_send, fwd_recv, bwd_send, bwd_recv,
    rel_sem, hand,
):
    g = lax.axis_index("gx")
    c = lax.axis_index("yz")
    other = 1 - c
    own = 2 * pairs
    rows = magnet.shape[1]
    cells = groups
    half = magnet.shape[2] // 2
    wide = 6 * half
    plane = math.gcd(couplers, 4)
    layers = groups // plane
    ring = couplers // 2
    first_q = (groups - couplers) // 2
    whole_tiles = own % 16 == 0

    coupler = jnp.logical_and(g >= first_q, g < first_q + couplers)
    m = jnp.clip(g - first_q, 0, couplers - 1)
    my_layer = g // plane
    low = 2 * my_layer < layers
    from_edge = jnp.where(low, my_layer, layers - 1 - my_layer)

    def layer_at(t):
        v = jnp.where(t <= from_edge, from_edge - t, t)
        return jnp.where(low, v, layers - 1 - v)

    def target(k):
        return layer_at(layers - 1 - k // plane) * plane + lax.rem(g + lax.rem(k, plane), plane)

    def forward_at(k):
        layer = k // plane
        layer = jnp.where(low, couplers // plane - 1 - layer, layer)
        return layer * plane + lax.rem(g + k % plane, plane)

    has_next, has_last = g < groups - 1, g > 0
    next_out = jnp.logical_and(has_next, jnp.logical_or(g + 1 < first_q, g + 1 >= first_q + couplers))
    last_out = jnp.logical_and(has_last, jnp.logical_or(g - 1 < first_q, g - 1 >= first_q + couplers))

    barrier = pltpu.get_barrier_semaphore()

    @pl.when(c == 0)
    def _():
        pl.semaphore_signal(barrier, inc=1, device_id=(g, 1), device_id_type=MESH)

    def greet(to):
        pl.semaphore_signal(barrier, inc=1, device_id=(to, 0), device_id_type=MESH)

    @pl.when(coupler)
    def _():
        for r in range(1, groups):
            greet(lax.rem(g + r, groups))

    @pl.when(jnp.logical_and(jnp.logical_not(coupler), has_next))
    def _():
        greet(g + 1)

    @pl.when(jnp.logical_and(jnp.logical_not(coupler), has_last))
    def _():
        greet(g - 1)

    loads = [
        pltpu.make_async_copy(magnet, mag.at[0], load_sem.at[0]),
        pltpu.make_async_copy(z_fwd, zf, load_sem.at[1]),
        pltpu.make_async_copy(y_fwd.at[c], yf, load_sem.at[2]),
    ]
    reverse = pltpu.make_async_copy(rev, rv, load_sem.at[3])
    late = [
        pltpu.make_async_copy(y_inv.at[c], yi, load_sem.at[4]),
        pltpu.make_async_copy(z_inv, zi, load_sem.at[5]),
    ]
    for copy in loads:
        copy.start()

    def newell_row(part, p):
        t = (2 * m + part) * pairs + p
        return (1 - c) * t + c * lax.rem(rows - t, rows)

    @pl.when(coupler)
    def _():
        for p in range(pairs):
            pltpu.make_async_copy(newell.at[newell_row(c, p)], nwl.at[c, p], load_sem.at[6]).start()
        reverse.start()

    for copy in late:
        copy.start()

    @pl.when(c == 1)
    def _():
        pl.semaphore_wait(barrier, 1)
        pl.semaphore_signal(hand.at[0], inc=1, device_id=(g, 0), device_id_type=MESH)

    @pl.when(c == 0)
    def _():
        pl.semaphore_wait(hand.at[0], 1)

    loads[0].wait()
    swap = [
        pltpu.make_async_remote_copy(
            src_ref=mag.at[0, comp],
            dst_ref=mag.at[1, comp],
            send_sem=pair_sem.at[0],
            recv_sem=swap_recv.at[comp],
            device_id=(g, other),
            device_id_type=MESH,
        )
        for comp in range(3)
    ]
    for copy in swap:
        copy.start()

    @pl.when(coupler)
    def _():
        for p in range(pairs):
            pltpu.make_async_remote_copy(
                src_ref=newell.at[newell_row(other, p)],
                dst_ref=nwl.at[c, p],
                send_sem=pair_sem.at[1],
                recv_sem=pair_sem.at[2],
                device_id=(g, other),
                device_id_type=MESH,
            ).start()

    far = pltpu.make_async_remote_copy(
        src_ref=nwl.at[c],
        dst_ref=nwl.at[other],
        send_sem=pair_sem.at[1],
        recv_sem=pair_sem.at[2],
        device_id=(g, other),
        device_id_type=MESH,
    )

    loads[1].wait()
    loads[2].wait()
    for side in range(2):
        for comp in range(3):
            if side == 1:
                swap[comp].wait_recv()
            zrow[pl.ds(side * rows, rows), pl.ds(2 * comp * half, 2 * half)] = jnp.dot(
                mag[side, comp], zf[...], preferred_element_type=F32
            ).astype(BF16)
            if side == 1:
                at = pl.ds(2 * comp * half, 2 * half)
                part = jnp.dot(yf[...], zrow[:, at], preferred_element_type=F32)
                if whole_tiles:
                    for i in range(couplers):
                        send[i, :, at] = part[i * own : (i + 1) * own].astype(BF16)
                else:
                    spec[:, at] = part
    if not whole_tiles:
        for i in range(couplers):
            send[i] = spec[pl.ds(i * own, own), :].astype(BF16)

    @pl.when(c == 0)
    def _():
        others = couplers - coupler.astype(jnp.int32) + next_out.astype(jnp.int32) + last_out.astype(jnp.int32)
        pl.semaphore_wait(barrier, 2 * others)
        pl.semaphore_signal(hand.at[1], inc=1, device_id=(g, 1), device_id_type=MESH)

    @pl.when(c == 1)
    def _():
        pl.semaphore_wait(hand.at[1], 1)

    def forward(to):
        return pltpu.make_async_remote_copy(
            src_ref=send.at[to],
            dst_ref=recv.at[g],
            send_sem=fwd_send.at[0],
            recv_sem=fwd_recv.at[my_layer],
            device_id=(first_q + to, c),
            device_id_type=MESH,
        )

    for k in range(couplers):
        @pl.when(first_q + forward_at(k) != g)
        def _():
            forward(forward_at(k)).start()

    def halo_copy(side):
        to = lax.rem(g + (1, groups - 1)[side], groups)
        return pltpu.make_async_remote_copy(
            src_ref=mag.at[0],
            dst_ref=halo.at[side],
            send_sem=halo_send.at[side],
            recv_sem=halo_recv.at[side],
            device_id=(to, c),
            device_id_type=MESH,
        )

    for side, inside in enumerate((has_next, has_last)):
        @pl.when(inside)
        def _():
            halo_copy(side).start()

    def waiter(ref, send_sem, recv_sem):
        return pltpu.make_async_remote_copy(
            src_ref=ref,
            dst_ref=ref,
            send_sem=send_sem,
            recv_sem=recv_sem,
            device_id=(g, other),
            device_id_type=MESH,
        )

    lane = lax.broadcasted_iota(jnp.int32, (pairs, half), 1)
    slot = lax.broadcasted_iota(jnp.int32, (pairs, half), 0)
    first_t = (2 * m + c) * pairs + slot
    al = first_t == 0
    ln = jnp.logical_and(lane == 0, first_t > 0)

    def wait_layer(layer):
        @pl.when(layer == my_layer)
        def _():
            waiter(recv.at[pl.ds(0, plane - 1)], fwd_send.at[0], fwd_recv.at[layer]).wait_recv()

        @pl.when(layer != my_layer)
        def _():
            waiter(recv.at[pl.ds(0, plane)], fwd_send.at[0], fwd_recv.at[layer]).wait_recv()

    def unpack(j):
        block = recv[j].astype(F32)
        for comp in range(3):
            re = block[:, 2 * comp * half : (2 * comp + 1) * half]
            im = block[:, (2 * comp + 1) * half : (2 * comp + 2) * half]
            cr, sr, ci, si = re[:pairs], re[pairs:], im[:pairs], im[pairs:]
            first_re = cr + jnp.where(jnp.logical_or(al, ln), 0.0, si)
            first_im = jnp.where(ln, 0.0, ci) - jnp.where(al, 0.0, sr)
            mirror_re = jnp.where(al, sr, jnp.where(ln, ci, cr - si))
            mirror_im = jnp.where(al, si, jnp.where(ln, -si, ci + sr))
            source[j, 2 * comp] = jnp.concatenate([first_re, mirror_re], axis=0)
            source[j, 2 * comp + 1] = jnp.concatenate([first_im, mirror_im], axis=0)

    def k_of(entry, d):
        start = pl.multiple_of((entry * cells + d) * own, own)
        return kern[pl.ds(start, own), :]

    def add_layer(layer, i):
        total = [acc[i, q] for q in range(6)]
        for p in range(plane):
            j = layer * plane + p
            d = jnp.abs(i - j)
            signed = jnp.where(i >= j, 4, 10)
            xx, yy, zz, yz = (k_of(e, d) for e in range(4))
            xy, xz = k_of(signed, d), k_of(signed + 1, d)
            xxi, yyi, zzi, yzi = (k_of(6 + e, d) for e in range(4))
            xr, xi, yr, yim, zr, zim = (source[j, q] for q in range(6))
            total[0] += xx * xr - xy * yim - xz * zim
            total[1] += xxi * xi + xy * yr + xz * zr
            total[2] += yy * yr + yz * zr - xy * xi
            total[3] += yyi * yim + yzi * zim + xy * xr
            total[4] += yz * yr + zz * zr - xz * xi
            total[5] += yzi * yim + zzi * zim + xz * xr
        return total

    def backward(i):
        return pltpu.make_async_remote_copy(
            src_ref=back.at[i],
            dst_ref=fields.at[c, m],
            send_sem=bwd_send.at[0],
            recv_sem=bwd_recv.at[m // ring],
            device_id=(i, c),
            device_id_type=MESH,
        )

    def prepare():
        recv[g] = send[m]
        for p in range(pairs):
            pltpu.make_async_copy(newell.at[newell_row(c, p)], nwl.at[c, p], load_sem.at[6]).wait()
        far.wait_recv()
        reverse.wait()
        table_rows = 6 * cells
        even_rows = 4 * cells
        lane0 = lax.broadcasted_iota(jnp.int32, (table_rows, half), 1) == 0
        even = lax.broadcasted_iota(jnp.int32, (table_rows, half), 0) < even_rows
        sign = jnp.where(even, 1.0, -1.0).astype(F32)
        for p in range(pairs):
            first = nwl[0, p].reshape(table_rows, 2 * half)
            mirror = nwl[1, p].reshape(table_rows, 2 * half)
            rev_first = jnp.dot(first, rv[...], preferred_element_type=F32)
            rev_mirror = jnp.dot(mirror, rv[...], preferred_element_type=F32)
            lo_first, hi_first = first[:, :half].astype(F32), first[:, half:].astype(F32)
            lo_mirror, hi_mirror = mirror[:, :half].astype(F32), mirror[:, half:].astype(F32)
            if p == 0:
                alone = ((2 * m + c) * pairs == 0).astype(F32)
                paired = 1.0 - alone
                of_first = alone * rev_first + paired * rev_mirror
                of_mirror = alone * rev_mirror + paired * rev_first
            else:
                of_first, of_mirror = rev_mirror, rev_first
            k_first = lo_first + sign * of_first
            k_mirror = lo_mirror + sign * of_mirror
            middle = hi_first + sign * hi_mirror
            if p == 0:
                i_first = jnp.where(lane0, alone * (2.0 * hi_first) + paired * k_first, k_first)
                i_mirror = jnp.where(lane0, alone * (2.0 * hi_mirror) + paired * middle, k_mirror)
                k_mirror = jnp.where(lane0, alone * k_mirror + paired * middle, k_mirror)
            else:
                k_mirror = jnp.where(lane0, middle, k_mirror)
                i_first, i_mirror = k_first, k_mirror
            for place, k_all, i_all in ((p, k_first, i_first), (pairs + p, k_mirror, i_mirror)):
                kern[pl.ds(place, table_rows, stride=own), :] = k_all
                kern[pl.ds(table_rows * own + place, even_rows, stride=own), :] = i_all[:even_rows]
                kern[pl.ds((table_rows + even_rows) * own + place, 2 * cells, stride=own), :] = -k_all[even_rows:]

    def couple():
        acc[...] = jnp.zeros(acc.shape, F32)

        def gather(t, carry):
            layer = layer_at(t)
            wait_layer(layer)
            for p in range(plane):
                unpack(layer * plane + p)

            def over(i, inner):
                total = add_layer(layer, i)
                for q in range(6):
                    acc[i, q] = total[q]
                return inner

            return lax.fori_loop(0, cells, over, carry)

        lax.fori_loop(0, layers - 1, gather, 0)
        layer = layer_at(layers - 1)
        wait_layer(layer)
        for p in range(plane):
            unpack(layer * plane + p)

        def finish(k, carry):
            i = target(k)
            total = add_layer(layer, i)
            for comp in range(3):
                re, im = total[2 * comp], total[2 * comp + 1]
                fr, mr, fi, mi = re[:pairs], re[pairs:], im[:pairs], im[pairs:]
                cos_re = fr + jnp.where(al, 0.0, jnp.where(ln, fr, mr))
                cos_im = jnp.where(ln, mr, fi) + jnp.where(al, 0.0, jnp.where(ln, mr, mi))
                sin_re = jnp.where(al, mr, jnp.where(ln, -fi, mi) - fi)
                sin_im = jnp.where(al, mi, jnp.where(ln, -mi, fr) - jnp.where(ln, mi, mr))
                back[i, :, pl.ds(2 * comp * half, half)] = jnp.concatenate([cos_re, sin_re], axis=0).astype(BF16)
                back[i, :, pl.ds((2 * comp + 1) * half, half)] = jnp.concatenate([cos_im, sin_im], axis=0).astype(BF16)
            before = target(jnp.maximum(k - 1, 0))

            @pl.when(jnp.logical_and(k > 0, before != g))
            def _():
                backward(before).start()

            return carry

        lax.fori_loop(0, cells, finish, 0)
        last = target(cells - 1)

        @pl.when(last != g)
        def _():
            backward(last).start()

        fields[c, m] = back[g]

    @pl.when(coupler)
    def _():
        prepare()

    for comp in range(3):
        full = jnp.concatenate([mag[0, comp], mag[1, comp]], axis=0).astype(F32)
        centre = full[:rows]
        total = pltpu.roll(full, 1, 0)[:rows] + pltpu.roll(full, 2 * rows - 1, 0)[:rows]
        total = total + pltpu.roll(centre, 1, 1) + pltpu.roll(centre, 2 * half - 1, 1)
        lap[comp] = total - 4.0 * centre

    @pl.when(coupler)
    def _():
        couple()

    for side, inside in enumerate((has_last, has_next)):
        @pl.when(inside)
        def _():
            halo_copy(side).wait_recv()

        @pl.when(jnp.logical_not(inside))
        def _():
            halo[side] = mag[0]

    for comp in range(3):
        centre = mag[0, comp].astype(F32)
        x_part = halo[0, comp].astype(F32) + halo[1, comp].astype(F32) - 2.0 * centre
        lap[comp] = EXCHANGE * (lap[comp] + x_part)

    def relay(n):
        return pltpu.make_async_remote_copy(
            src_ref=fields.at[c, pl.ds(n * ring, ring)],
            dst_ref=fields.at[c, pl.ds(n * ring, ring)],
            send_sem=rel_sem.at[0],
            recv_sem=rel_sem.at[1],
            device_id=(g, other),
            device_id_type=MESH,
        )

    rings = couplers // ring
    for k in range(rings):
        n = jnp.where(low, k, rings - 1 - k)
        mine = jnp.logical_and(coupler, m // ring == n)
        if ring > 1:
            @pl.when(mine)
            def _():
                waiter(fields.at[c, pl.ds(0, ring - 1)], bwd_send.at[0], bwd_recv.at[n]).wait_recv()

        @pl.when(jnp.logical_not(mine))
        def _():
            waiter(fields.at[c, pl.ds(0, ring)], bwd_send.at[0], bwd_recv.at[n]).wait_recv()

        relay(n).start()

    for copy in late:
        copy.wait()
    waiter(fields.at[other], rel_sem.at[0], rel_sem.at[1]).wait_recv()

    if whole_tiles:
        modes = fields[...].reshape(2 * couplers * own, wide)
    else:
        for part in range(2):
            for i in range(couplers):
                stack[pl.ds((part * couplers + i) * own, own), :] = fields[part, i].astype(F32)
        modes = stack[...].astype(BF16)
    scale = 1.0 / (2 * rows * 2 * half)
    for comp in range(3):
        at = slice(2 * comp * half, 2 * (comp + 1) * half)
        g_rows = jnp.dot(yi[...], modes[:, at], preferred_element_type=F32).astype(BF16)
        demag = jnp.dot(g_rows, zi[...], preferred_element_type=F32) * scale
        out[comp] = (demag + lap[comp]).astype(BF16)

    waiter(mag.at[0], pair_sem.at[0], pair_sem.at[2]).wait_send()
    waiter(fields.at[c], rel_sem.at[0], rel_sem.at[1]).wait_send()

    @pl.when(coupler)
    def _():
        far.wait_send()
        waiter(send.at[pl.ds(0, couplers - 1)], fwd_send.at[0], fwd_recv.at[0]).wait_send()
        waiter(back.at[pl.ds(0, groups - 1)], bwd_send.at[0], bwd_recv.at[0]).wait_send()

    @pl.when(jnp.logical_not(coupler))
    def _():
        waiter(send, fwd_send.at[0], fwd_recv.at[0]).wait_send()

    for side, inside in enumerate((has_next, has_last)):
        @pl.when(inside)
        def _():
            halo_copy(side).wait_send()


def on_device(magnet, newell, *consts):
    rows, _, x_cells, z_total = magnet.shape
    groups = lax.axis_size("gx")
    parts = lax.axis_size("yz")
    assert x_cells == 1 and parts == 2
    couplers = groups // 2
    y_total = rows * parts
    pairs = y_total // (couplers * parts * 2)
    own = 2 * pairs
    half = z_total // 2
    wide = 3 * z_total
    layers = groups // math.gcd(couplers, 4)
    any_ref = pl.BlockSpec(memory_space=pl.ANY)
    dma = pltpu.SemaphoreType.DMA
    planes = jnp.transpose(magnet[:, :, 0, :], (1, 0, 2))
    field = pl.pallas_call(
        functools.partial(kernel, groups, couplers, pairs),
        out_shape=pltpu.VMEM(planes.shape, BF16),
        in_specs=[any_ref] * 7,
        out_specs=pl.BlockSpec(memory_space=pltpu.VMEM),
        scratch_shapes=[
            pltpu.VMEM((2, 3, rows, z_total), BF16),
            pltpu.VMEM((2, pairs, 6, groups, z_total), BF16),
            pltpu.VMEM((rows, y_total), BF16),
            pltpu.VMEM((rows, y_total), BF16),
            pltpu.VMEM((z_total, z_total), BF16),
            pltpu.VMEM((z_total, z_total), BF16),
            pltpu.VMEM((z_total, half), BF16),
            pltpu.VMEM((2, 3, rows, z_total), BF16),
            pltpu.VMEM((y_total, wide), BF16),
            pltpu.VMEM((rows, wide), F32),
            pltpu.VMEM((couplers, own, wide), BF16),
            pltpu.VMEM((groups, own, wide), BF16),
            pltpu.VMEM((12 * groups * own, half), F32),
            pltpu.VMEM((groups, 6, own, half), F32),
            pltpu.VMEM((groups, 6, own, half), F32),
            pltpu.VMEM((groups, own, wide), BF16),
            pltpu.VMEM((2, couplers, own, wide), BF16),
            pltpu.VMEM((y_total, wide), F32),
            pltpu.VMEM((3, rows, z_total), F32),
            dma((7,)),
            dma((3,)),
            dma((3,)),
            dma((2,)),
            dma((2,)),
            dma((1,)),
            dma((layers,)),
            dma((1,)),
            dma((2,)),
            dma((2,)),
            pltpu.SemaphoreType.REGULAR((2,)),
        ],
        compiler_params=pltpu.CompilerParams(collective_id=0, has_side_effects=True),
    )(planes, newell, *consts)
    return jnp.transpose(field, (1, 0, 2))[:, :, None, :]


def solution(mesh):
    groups, parts = mesh.shape["gx"], mesh.shape["yz"]

    def run(magnet, newell):
        consts = tables(groups // 2, parts, magnet.shape[0], magnet.shape[3])
        body = lambda m, n: on_device(m, n, *[jnp.asarray(t) for t in consts])
        return jax.shard_map(
            body,
            mesh=mesh,
            in_specs=(P("yz", None, "gx", None), P("yz", None, None, None)),
            out_specs=P("yz", None, "gx", None),
            check_vma=False,
        )(magnet, newell)

    return run
```

time: 24.8 us -> 24.9 us (level)
  no operation moved by 1% of the time
where the time goes in v1:
time: 24.9 us; the launch traced here: 24.6 us
  Pallas kernels  23.9 us (96%)
  local copies, waits for them, and re-layouts  0.68 us (3%)
    pallas_call x1, Pallas kernels, on_device(): pl.pallas_call(functools.partial(kernel, groups, couplers, pairs), out_sh...  23.9 us
    unnamed x1, local copies, waits for them, and re-layouts  0.68 us

profile of v1, /device:TPU:0, one launch (start us, length us, event | category | flops | bytes accessed | tf_op | source)
XLA Modules:
  0.0 24.6 jit_solution(16202346967846606673)
XLA Ops:
  0.0 23.9 %shard_map.73 = bf16[3,128,256]{2,1,0:T(8,128)(2,1)S(1)} custom-call(bf16[3,128,256]{2,1,0:T(8,128)(2,1)} %bitcast.9, bf16[128,6,16,256]{3,2,1,0:T(8,128)(2,1)} %newell.1, bf16[2,128,256]{2,1,0:T(8,128)(2,1)} %constant.10.clone.y_fwd, bf16[2,128,256]{2,1,0:T(8,128)(2,1)} %constant.11.clone.y_inv, bf16[256,256]{1,0:T(8,128)(2,1)} %constant.12.clone.z_fwd, ...), custom_call_target="tpu_custom_call" | custom-call | tf_op jit(solution)/shard_map/pallas_call | solution.py:523
  23.9 0.7 %copy.10 = bf16[128,3,1,256]{3,0,2,1:T(8,128)(2,1)} copy(bf16[128,3,1,256]{3,0,2,1:T(8,128)(2,1)S(1)} %bitcast.8) | data formatting | bytes 393216

commit v2 on v1

v2 whole, which is shorter than its diff:
```python
import functools
import math

import jax
import jax.numpy as jnp
import ml_dtypes
import numpy as np
from jax import lax
from jax.experimental import pallas as pl
from jax.experimental.pallas import tpu as pltpu
from jax.sharding import PartitionSpec as P

EXCHANGE = 0.2
F32 = jnp.float32
BF16 = jnp.bfloat16
MESH = pl.DeviceIdType.MESH


def tables(groups, parts, y_total, z_total):
    pairs = y_total // (groups * parts * 2)
    rows = y_total // parts
    half_y = y_total // 2

    def trig(k, n, length):
        angle = (k[:, None] * n[None, :] % length) * (2.0 * math.pi / length)
        return np.cos(angle), np.sin(angle)

    def y_rows(part, n):
        blocks = []
        for m in range(groups):
            t = (m * parts + part) * pairs + np.arange(pairs)
            cos, sin = trig(t, n, y_total)
            if t[0] == 0:
                sin[0] = trig(np.array([half_y]), n, y_total)[0][0]
            blocks += [cos, sin]
        return np.concatenate(blocks)

    half = z_total // 2
    cos, sin = trig(np.arange(z_total), np.arange(half), z_total)
    alternate = np.cos(math.pi * np.arange(z_total))
    z_fwd = np.concatenate([cos, -sin], axis=1)
    z_fwd[:, half] = alternate
    z_inv = -np.concatenate([cos, -sin], axis=1).T
    z_inv[0] = -0.5
    z_inv[half] = -0.5 * alternate
    reverse = np.zeros((z_total, half))
    for k in range(half):
        reverse[-k % z_total, k] = 1.0
    forward, inverse = [], []
    for part in range(parts):
        own_first = (np.arange(y_total) + part * rows) % y_total
        forward.append(y_rows(part, own_first))
        inverse.append(np.concatenate([y_rows(other, own_first[:rows]) for other in range(parts)]).T)
    cast = lambda a: np.asarray(a, np.float32).astype(ml_dtypes.bfloat16)
    return cast(np.stack(forward)), cast(np.stack(inverse)), cast(z_fwd), cast(z_inv), cast(reverse)


def kernel(
    groups, pairs, magnet, newell, y_fwd, y_inv, z_fwd, z_inv, rev, out,
    mag, nwl, yf, yi, zf, zi, rv, zrow, spec, send, recv, kern, acc, back, fields, stack,
    lap, load_sem, swap_recv, pair_sem, fwd_send, fwd_recv, bwd_send, bwd_recv,
    rel_sem, hand,
):
    g = lax.axis_index("gx")
    c = lax.axis_index("yz")
    other = 1 - c
    own = 2 * pairs
    rows = magnet.shape[1]
    cells = groups
    half = magnet.shape[2] // 2
    wide = 6 * half
    plane = math.gcd(groups, 4)
    layers = groups // plane
    whole_tiles = own % 8 == 0

    last = groups - 1
    extra = groups // 4 + 1
    active = (g != last, g == extra)
    blocks = (g, last)

    def owner(b):
        return jnp.where(b == last, extra, b)

    my_layer = g // plane
    low = 2 * my_layer < layers
    from_edge = jnp.where(low, my_layer, layers - 1 - my_layer)

    def layer_at(t):
        v = jnp.where(t <= from_edge, from_edge - t, t)
        return jnp.where(low, v, layers - 1 - v)

    def target(k):
        return layer_at(layers - 1 - k // plane) * plane + lax.rem(g + lax.rem(k, plane), plane)

    barrier = pltpu.get_barrier_semaphore()

    @pl.when(c == 0)
    def _():
        pl.semaphore_signal(barrier, inc=1, device_id=(g, 1), device_id_type=MESH)

    def greet(to):
        pl.semaphore_signal(barrier, inc=1, device_id=(to, 0), device_id_type=MESH)

    @pl.when(g != last)
    def _():
        for r in range(1, groups):
            greet(lax.rem(g + r, groups))

    loads = [
        pltpu.make_async_copy(magnet, mag.at[0], load_sem.at[0]),
        pltpu.make_async_copy(z_fwd, zf, load_sem.at[1]),
        pltpu.make_async_copy(y_fwd.at[c], yf, load_sem.at[2]),
    ]
    reverse = pltpu.make_async_copy(rev, rv, load_sem.at[3])
    late = [
        pltpu.make_async_copy(y_inv.at[c], yi, load_sem.at[4]),
        pltpu.make_async_copy(z_inv, zi, load_sem.at[5]),
    ]
    for copy in loads:
        copy.start()

    def newell_row(slot, part, p):
        t = (2 * blocks[slot] + part) * pairs + p
        return (1 - c) * t + c * lax.rem(rows - t, rows)

    def near(slot, p):
        at = slot * pairs + p
        return pltpu.make_async_copy(newell.at[newell_row(slot, c, p)], nwl.at[c, at], load_sem.at[6 + slot])

    for slot in range(2):
        @pl.when(active[slot])
        def _():
            for p in range(pairs):
                near(slot, p).start()

    @pl.when(g != last)
    def _():
        reverse.start()

    for copy in late:
        copy.start()

    @pl.when(c == 1)
    def _():
        pl.semaphore_wait(barrier, 1)
        pl.semaphore_signal(hand.at[0], inc=1, device_id=(g, 0), device_id_type=MESH)

    @pl.when(c == 0)
    def _():
        pl.semaphore_wait(hand.at[0], 1)

    loads[0].wait()
    swap = [
        pltpu.make_async_remote_copy(
            src_ref=mag.at[0, comp],
            dst_ref=mag.at[1, comp],
            send_sem=pair_sem.at[0],
            recv_sem=swap_recv.at[comp],
            device_id=(g, other),
            device_id_type=MESH,
        )
        for comp in range(3)
    ]
    for copy in swap:
        copy.start()

    def far(slot, p, count):
        at = pl.ds(slot * pairs + p, count)
        row = newell_row(slot, other, p)
        return pltpu.make_async_remote_copy(
            src_ref=newell.at[pl.ds(row, 1)] if count == 1 else nwl.at[c, at],
            dst_ref=nwl.at[c, at],
            send_sem=pair_sem.at[1 + slot],
            recv_sem=pair_sem.at[3 + slot],
            device_id=(g, other),
            device_id_type=MESH,
        )

    for slot in range(2):
        @pl.when(active[slot])
        def _():
            for p in range(pairs):
                far(slot, p, 1).start()

    loads[1].wait()
    loads[2].wait()
    for side in range(2):
        for comp in range(3):
            if side == 1:
                swap[comp].wait_recv()
            zrow[pl.ds(side * rows, rows), pl.ds(2 * comp * half, 2 * half)] = jnp.dot(
                mag[side, comp], zf[...], preferred_element_type=F32
            ).astype(BF16)
            if side == 1:
                at = pl.ds(2 * comp * half, 2 * half)
                part = jnp.dot(yf[...], zrow[:, at], preferred_element_type=F32)
                if whole_tiles:
                    for i in range(groups):
                        send[i, :, at] = part[i * own : (i + 1) * own].astype(BF16)
                else:
                    spec[:, at] = part
    if not whole_tiles:
        for i in range(groups):
            send[i] = spec[pl.ds(i * own, own), :].astype(BF16)

    @pl.when(c == 0)
    def _():
        pl.semaphore_wait(barrier, 2 * (last - (g != last).astype(jnp.int32)))
        pl.semaphore_signal(hand.at[1], inc=1, device_id=(g, 1), device_id_type=MESH)

    @pl.when(c == 1)
    def _():
        pl.semaphore_wait(hand.at[1], 1)

    def forward(b):
        slot = (b == last).astype(jnp.int32)
        return pltpu.make_async_remote_copy(
            src_ref=send.at[b],
            dst_ref=recv.at[slot, g],
            send_sem=fwd_send.at[0],
            recv_sem=fwd_recv.at[slot * layers + my_layer],
            device_id=(owner(b), c),
            device_id_type=MESH,
        )

    for k in range(groups):
        b = target(k)

        @pl.when(owner(b) != g)
        def _():
            forward(b).start()

    def waiter(ref, send_sem, recv_sem):
        return pltpu.make_async_remote_copy(
            src_ref=ref,
            dst_ref=ref,
            send_sem=send_sem,
            recv_sem=recv_sem,
            device_id=(g, other),
            device_id_type=MESH,
        )

    lane = lax.broadcasted_iota(jnp.int32, (own, half), 1)
    row = lax.broadcasted_iota(jnp.int32, (own, half), 0)
    top = row < pairs

    def masks(slot):
        first_t = (2 * blocks[slot] + c) * pairs + lax.rem(row, pairs)
        al = first_t == 0
        ln = jnp.logical_and(lane == 0, first_t > 0)
        return al, jnp.logical_or(al, ln), jnp.logical_and(ln, jnp.logical_not(top))

    def flip(v):
        return jnp.concatenate([v[pairs:], v[:pairs]], axis=0)

    def wait_layer(slot, layer):
        sem = fwd_recv.at[slot * layers + layer]

        @pl.when(layer == my_layer)
        def _():
            waiter(recv.at[slot, pl.ds(0, plane - 1)], fwd_send.at[0], sem).wait_recv()

        @pl.when(layer != my_layer)
        def _():
            waiter(recv.at[slot, pl.ds(0, plane)], fwd_send.at[0], sem).wait_recv()

    def unpack(slot, j):
        al, special, ln_low = masks(slot)
        block = recv[slot, j].astype(F32)
        parts = []
        for comp in range(3):
            re = block[:, 2 * comp * half : (2 * comp + 1) * half]
            im = block[:, (2 * comp + 1) * half : (2 * comp + 2) * half]
            re_f, im_f = flip(re), flip(im)
            new_re = jnp.where(top, re + im_f, re_f - im)
            new_im = jnp.where(top, im - re_f, im_f + re)
            lone_re = jnp.where(ln_low, im_f, re)
            lone_im = jnp.where(al, im, -jnp.where(top, re_f, im))
            parts.append(jnp.where(special, lone_re, new_re))
            parts.append(jnp.where(special, lone_im, new_im))
        return parts

    def k_of(slot, entry, d):
        start = pl.multiple_of(((slot * 12 + entry) * cells + d) * own, own)
        return kern[pl.ds(start, own), :]

    def add_layer(slot, layer, sources, i):
        total = [acc[slot, i, q] for q in range(6)]
        for p in range(plane):
            j = layer * plane + p
            d = jnp.abs(i - j)
            signed = jnp.where(i >= j, 4, 10)
            xx, yy, zz, yz = (k_of(slot, e, d) for e in range(4))
            xy, xz = k_of(slot, signed, d), k_of(slot, signed + 1, d)
            xxi, yyi, zzi, yzi = (k_of(slot, 6 + e, d) for e in range(4))
            xr, xi, yr, yim, zr, zim = sources[p]
            total[0] += xx * xr - xy * yim - xz * zim
            total[1] += xxi * xi + xy * yr + xz * zr
            total[2] += yy * yr + yz * zr - xy * xi
            total[3] += yyi * yim + yzi * zim + xy * xr
            total[4] += yz * yr + zz * zr - xz * xi
            total[5] += yzi * yim + zzi * zim + xz * xr
        return total

    def backward(slot, i):
        return pltpu.make_async_remote_copy(
            src_ref=back.at[slot, i],
            dst_ref=fields.at[c, blocks[slot]],
            send_sem=bwd_send.at[0],
            recv_sem=bwd_recv.at[blocks[slot] // plane],
            device_id=(i, c),
            device_id_type=MESH,
        )

    def prepare(slot):
        recv[slot, g] = send[blocks[slot]]
        for p in range(pairs):
            near(slot, p).wait()
        far(slot, 0, pairs).wait_recv()
        table_rows = 6 * cells
        even_rows = 4 * cells
        lane0 = lax.broadcasted_iota(jnp.int32, (table_rows, half), 1) == 0
        even = lax.broadcasted_iota(jnp.int32, (table_rows, half), 0) < even_rows
        sign = jnp.where(even, 1.0, -1.0).astype(F32)
        row_of = lax.broadcasted_iota(jnp.int32, (table_rows, half), 0)
        diagonal = functools.reduce(jnp.logical_or, [row_of == entry * cells + 1 for entry in range(3)])
        neighbour = jnp.where(diagonal, -2.0 * EXCHANGE, 0.0).astype(F32)
        base = slot * 12 * cells * own
        for p in range(pairs):
            first = nwl[0, slot * pairs + p].reshape(table_rows, 2 * half)
            mirror = nwl[1, slot * pairs + p].reshape(table_rows, 2 * half)
            rev_first = jnp.dot(first, rv[...], preferred_element_type=F32)
            rev_mirror = jnp.dot(mirror, rv[...], preferred_element_type=F32)
            lo_first, hi_first = first[:, :half].astype(F32), first[:, half:].astype(F32)
            lo_mirror, hi_mirror = mirror[:, :half].astype(F32), mirror[:, half:].astype(F32)
            if p == 0:
                alone = ((2 * blocks[slot] + c) * pairs == 0).astype(F32)
                paired = 1.0 - alone
                of_first = alone * rev_first + paired * rev_mirror
                of_mirror = alone * rev_mirror + paired * rev_first
            else:
                of_first, of_mirror = rev_mirror, rev_first
            k_first = lo_first + sign * of_first
            k_mirror = lo_mirror + sign * of_mirror
            middle = hi_first + sign * hi_mirror
            if p == 0:
                i_first = jnp.where(lane0, alone * (2.0 * hi_first) + paired * k_first, k_first)
                i_mirror = jnp.where(lane0, alone * (2.0 * hi_mirror) + paired * middle, k_mirror)
                k_mirror = jnp.where(lane0, alone * k_mirror + paired * middle, k_mirror)
            else:
                k_mirror = jnp.where(lane0, middle, k_mirror)
                i_first, i_mirror = k_first, k_mirror
            for place, k_all, i_all in ((p, k_first, i_first), (pairs + p, k_mirror, i_mirror)):
                k_all, i_all = k_all + neighbour, i_all + neighbour
                kern[pl.ds(base + place, table_rows, stride=own), :] = k_all
                kern[pl.ds(base + table_rows * own + place, even_rows, stride=own), :] = i_all[:even_rows]
                kern[pl.ds(base + (table_rows + even_rows) * own + place, 2 * cells, stride=own), :] = -k_all[even_rows:]
        acc[slot] = jnp.zeros(acc.shape[1:], F32)

    def gather(slot, layer):
        wait_layer(slot, layer)
        sources = [unpack(slot, layer * plane + p) for p in range(plane)]

        def over(n, inner):
            for p in range(plane):
                i = n * plane + p
                total = add_layer(slot, layer, sources, i)
                for q in range(6):
                    acc[slot, i, q] = total[q]
            return inner

        lax.fori_loop(0, layers, over, 0)

    def finish(slot, layer):
        wait_layer(slot, layer)
        sources = [unpack(slot, layer * plane + p) for p in range(plane)]
        al, special, _ = masks(slot)

        def dispatch(n):
            for p in range(plane):
                i = target(n * plane + p)

                @pl.when(i != g)
                def _():
                    backward(slot, i).start()

        def over(n, carry):
            for p in range(plane):
                i = target(n * plane + p)
                spread(i, add_layer(slot, layer, sources, i))

            @pl.when(n > 0)
            def _():
                dispatch(jnp.maximum(n - 1, 0))

            return carry

        def spread(i, total):
            for comp in range(3):
                re, im = total[2 * comp], total[2 * comp + 1]
                re_f, im_f = flip(re), flip(im)
                new_re = jnp.where(top, re + re_f, im - im_f)
                new_im = jnp.where(top, im + im_f, re_f - re)
                lone_re = jnp.where(al, re, 2.0 * jnp.where(top, re, -im_f))
                lone_im = jnp.where(al, im, 2.0 * jnp.where(top, re_f, -im))
                new_re = jnp.where(special, lone_re, new_re)
                new_im = jnp.where(special, lone_im, new_im)
                back[slot, i, :, pl.ds(2 * comp * half, half)] = new_re.astype(BF16)
                back[slot, i, :, pl.ds((2 * comp + 1) * half, half)] = new_im.astype(BF16)

        lax.fori_loop(0, layers, over, 0)
        dispatch(layers - 1)
        fields[c, blocks[slot]] = back[slot, g]

    @pl.when(g != last)
    def _():
        reverse.wait()

    for slot in range(2):
        @pl.when(active[slot])
        def _():
            prepare(slot)

    beside = (g > 0).astype(F32) + (g < groups - 1).astype(F32)
    for comp in range(3):
        full = jnp.concatenate([mag[0, comp], mag[1, comp]], axis=0).astype(F32)
        centre = full[:rows]
        total = pltpu.roll(full, 1, 0)[:rows] + pltpu.roll(full, 2 * rows - 1, 0)[:rows]
        total = total + pltpu.roll(centre, 1, 1) + pltpu.roll(centre, 2 * half - 1, 1)
        lap[comp] = EXCHANGE * (total - (4.0 + beside) * centre)

    def step(t, carry):
        for slot in range(2):
            @pl.when(active[slot])
            def _():
                gather(slot, layer_at(t))
        return carry

    lax.fori_loop(0, layers - 1, step, 0)
    for slot in range(2):
        @pl.when(active[slot])
        def _():
            finish(slot, layer_at(layers - 1))

    def relay(n):
        return pltpu.make_async_remote_copy(
            src_ref=fields.at[c, pl.ds(n * plane, plane)],
            dst_ref=fields.at[c, pl.ds(n * plane, plane)],
            send_sem=rel_sem.at[0],
            recv_sem=rel_sem.at[1],
            device_id=(g, other),
            device_id_type=MESH,
        )

    for k in range(layers):
        n = layer_at(k)
        mine = jnp.logical_and(g != last, n == my_layer)
        local = mine.astype(jnp.int32) + jnp.logical_and(g == extra, n == last // plane).astype(jnp.int32)
        for count in range(plane - 2, plane + 1):
            if count > 0:
                @pl.when(plane - local == count)
                def _():
                    waiter(fields.at[c, pl.ds(0, count)], bwd_send.at[0], bwd_recv.at[n]).wait_recv()

        relay(n).start()

    for copy in late:
        copy.wait()
    waiter(fields.at[other], rel_sem.at[0], rel_sem.at[1]).wait_recv()

    if whole_tiles:
        modes = fields[...].reshape(2 * groups * own, wide)
    else:
        for part in range(2):
            for i in range(groups):
                stack[pl.ds((part * groups + i) * own, own), :] = fields[part, i].astype(F32)
        modes = stack[...].astype(BF16)
    scale = 1.0 / (2 * rows * 2 * half)
    for comp in range(3):
        at = slice(2 * comp * half, 2 * (comp + 1) * half)
        g_rows = jnp.dot(yi[...], modes[:, at], preferred_element_type=F32).astype(BF16)
        demag = jnp.dot(g_rows, zi[...], preferred_element_type=F32) * scale
        out[comp] = (demag + lap[comp]).astype(BF16)

    waiter(mag.at[0], pair_sem.at[0], swap_recv.at[0]).wait_send()
    waiter(fields.at[c], rel_sem.at[0], rel_sem.at[1]).wait_send()
    for slot in range(2):
        @pl.when(active[slot])
        def _():
            far(slot, 0, pairs).wait_send()
            waiter(back.at[slot, pl.ds(0, groups - 1)], bwd_send.at[0], bwd_recv.at[0]).wait_send()

    kept = active[0].astype(jnp.int32) + active[1].astype(jnp.int32)
    for count in range(3):
        @pl.when(kept == count)
        def _():
            waiter(send.at[pl.ds(0, groups - count)], fwd_send.at[0], fwd_recv.at[0]).wait_send()


def on_device(magnet, newell, *consts):
    rows, _, x_cells, z_total = magnet.shape
    groups = lax.axis_size("gx")
    parts = lax.axis_size("yz")
    assert x_cells == 1 and parts == 2
    y_total = rows * parts
    pairs = y_total // (groups * parts * 2)
    own = 2 * pairs
    half = z_total // 2
    wide = 3 * z_total
    layers = groups // math.gcd(groups, 4)
    any_ref = pl.BlockSpec(memory_space=pl.ANY)
    dma = pltpu.SemaphoreType.DMA
    planes = jnp.transpose(magnet[:, :, 0, :], (1, 0, 2))
    field = pl.pallas_call(
        functools.partial(kernel, groups, pairs),
        out_shape=pltpu.VMEM(planes.shape, BF16),
        in_specs=[any_ref] * 7,
        out_specs=pl.BlockSpec(memory_space=pltpu.VMEM),
        scratch_shapes=[
            pltpu.VMEM((2, 3, rows, z_total), BF16),
            pltpu.VMEM((2, 2 * pairs, 6, groups, z_total), BF16),
            pltpu.VMEM((rows, y_total), BF16),
            pltpu.VMEM((rows, y_total), BF16),
            pltpu.VMEM((z_total, z_total), BF16),
            pltpu.VMEM((z_total, z_total), BF16),
            pltpu.VMEM((z_total, half), BF16),
            pltpu.VMEM((y_total, wide), BF16),
            pltpu.VMEM((rows, wide), F32),
            pltpu.VMEM((groups, own, wide), BF16),
            pltpu.VMEM((2, groups, own, wide), BF16),
            pltpu.VMEM((2 * 12 * groups * own, half), F32),
            pltpu.VMEM((2, groups, 6, own, half), F32),
            pltpu.VMEM((2, groups, own, wide), BF16),
            pltpu.VMEM((2, groups, own, wide), BF16),
            pltpu.VMEM((y_total, wide), F32),
            pltpu.VMEM((3, rows, z_total), F32),
            dma((8,)),
            dma((3,)),
            dma((5,)),
            dma((1,)),
            dma((2 * layers,)),
            dma((1,)),
            dma((layers,)),
            dma((2,)),
            pltpu.SemaphoreType.REGULAR((2,)),
        ],
        compiler_params=pltpu.CompilerParams(collective_id=0, has_side_effects=True),
    )(planes, newell, *consts)
    return jnp.transpose(field, (1, 0, 2))[:, :, None, :]


def solution(mesh):
    groups, parts = mesh.shape["gx"], mesh.shape["yz"]

    def run(magnet, newell):
        consts = tables(groups, parts, magnet.shape[0], magnet.shape[3])
        body = lambda m, n: on_device(m, n, *[jnp.asarray(t) for t in consts])
        return jax.shard_map(
            body,
            mesh=mesh,
            in_specs=(P("yz", None, "gx", None), P("yz", None, None, None)),
            out_specs=P("yz", None, "gx", None),
            check_vma=False,
        )(magnet, newell)

    return run
```

time: 24.9 us -> 23 us (0.924)
  Pallas kernels: 23.9 us -> 21.8 us
    pallas_call x1, Pallas kernels: 23.9 us -> 21.8 us  [on_device(): pl.pallas_call(functools.partial(kernel, groups, pairs), out_shape=pltpu....]
where the time goes in v2:
time: 23 us; the launch traced here: 22.5 us
  Pallas kernels  21.8 us (95%)
  local copies, waits for them, and re-layouts  0.68 us (3%)
    pallas_call x1, Pallas kernels, on_device(): pl.pallas_call(functools.partial(kernel, groups, pairs), out_shape=pltpu....  21.8 us
    unnamed x1, local copies, waits for them, and re-layouts  0.68 us

profile of v2, /device:TPU:0, one launch (start us, length us, event | category | flops | bytes accessed | tf_op | source)
XLA Modules:
  0.0 22.5 jit_solution(15678484647152807505)
XLA Ops:
  0.0 21.8 %shard_map.73 = bf16[3,128,256]{2,1,0:T(8,128)(2,1)S(1)} custom-call(bf16[3,128,256]{2,1,0:T(8,128)(2,1)} %bitcast.9, bf16[128,6,16,256]{3,2,1,0:T(8,128)(2,1)} %newell.1, bf16[2,128,256]{2,1,0:T(8,128)(2,1)} %constant.10.clone.y_fwd, bf16[2,128,256]{2,1,0:T(8,128)(2,1)} %constant.11.clone.y_inv, bf16[256,256]{1,0:T(8,128)(2,1)} %constant.12.clone.z_fwd, ...), custom_call_target="tpu_custom_call" | custom-call | tf_op jit(solution)/shard_map/pallas_call | solution.py:514
  21.8 0.7 %copy.10 = bf16[128,3,1,256]{3,0,2,1:T(8,128)(2,1)} copy(bf16[128,3,1,256]{3,0,2,1:T(8,128)(2,1)S(1)} %bitcast.8) | data formatting | bytes 393216

commit v3 on v2

v3 whole, which is shorter than its diff:
```python
import functools
import math

import jax
import jax.numpy as jnp
import ml_dtypes
import numpy as np
from jax import lax
from jax.experimental import pallas as pl
from jax.experimental.pallas import tpu as pltpu
from jax.sharding import PartitionSpec as P

EXCHANGE = 0.2
F32 = jnp.float32
BF16 = jnp.bfloat16
MESH = pl.DeviceIdType.MESH


def tables(groups, parts, y_total, z_total):
    pairs = y_total // (groups * parts * 2)
    rows = y_total // parts
    half_y = y_total // 2

    def trig(k, n, length):
        angle = (k[:, None] * n[None, :] % length) * (2.0 * math.pi / length)
        return np.cos(angle), np.sin(angle)

    def y_rows(part, n):
        blocks = []
        for m in range(groups):
            t = (m * parts + part) * pairs + np.arange(pairs)
            cos, sin = trig(t, n, y_total)
            if t[0] == 0:
                sin[0] = trig(np.array([half_y]), n, y_total)[0][0]
            blocks += [cos, sin]
        return np.concatenate(blocks)

    half = z_total // 2
    cos, sin = trig(np.arange(z_total), np.arange(half), z_total)
    alternate = np.cos(math.pi * np.arange(z_total))
    z_fwd = np.concatenate([cos, -sin], axis=1)
    z_fwd[:, half] = alternate
    z_inv = -np.concatenate([cos, -sin], axis=1).T
    z_inv[0] = -0.5
    z_inv[half] = -0.5 * alternate
    reverse = np.zeros((z_total, half))
    for k in range(half):
        reverse[-k % z_total, k] = 1.0
    forward, inverse = [], []
    for part in range(parts):
        own_first = (np.arange(y_total) + part * rows) % y_total
        forward.append(y_rows(part, own_first))
        inverse.append(np.concatenate([y_rows(other, own_first[:rows]) for other in range(parts)]).T)
    cast = lambda a: np.asarray(a, np.float32).astype(ml_dtypes.bfloat16)
    return cast(np.stack(forward)), cast(np.stack(inverse)), cast(z_fwd), cast(z_inv), cast(reverse)


def kernel(
    groups, pairs, magnet, newell, y_fwd, y_inv, z_fwd, z_inv, rev, out,
    mag, nwl, yf, yi, zf, zi, rv, zrow, spec, send, recv, kern, acc, back, fields, stack,
    lap, load_sem, near_sem, swap_recv, pair_sem, fwd_send, fwd_recv, bwd_send, bwd_recv,
    rel_sem, hand,
):
    g = lax.axis_index("gx")
    c = lax.axis_index("yz")
    other = 1 - c
    own = 2 * pairs
    rows = magnet.shape[1]
    cells = groups
    half = magnet.shape[2] // 2
    wide = 6 * half
    plane = math.gcd(groups, 4)
    layers = groups // plane
    whole_tiles = own % 8 == 0

    my_layer = g // plane
    low = 2 * my_layer < layers
    from_edge = jnp.where(low, my_layer, layers - 1 - my_layer)

    def layer_at(t):
        v = jnp.where(t <= from_edge, from_edge - t, t)
        return jnp.where(low, v, layers - 1 - v)

    def target(k):
        return lax.rem(g + k, groups)

    def relay_at(t):
        return layer_at(t)

    def group_at(t):
        return lax.rem(my_layer + layers - t, layers)

    barrier = pltpu.get_barrier_semaphore()
    loads = [
        pltpu.make_async_copy(magnet.at[comp], mag.at[0, comp], load_sem.at[comp]) for comp in range(3)
    ]
    tabs = [
        pltpu.make_async_copy(z_fwd, zf, load_sem.at[3]),
        pltpu.make_async_copy(y_fwd.at[c], yf, load_sem.at[4]),
    ]
    late = [
        pltpu.make_async_copy(rev, rv, load_sem.at[5]),
        pltpu.make_async_copy(y_inv.at[c], yi, load_sem.at[6]),
        pltpu.make_async_copy(z_inv, zi, load_sem.at[7]),
    ]
    for copy in loads:
        copy.start()

    @pl.when(c == 0)
    def _():
        pl.semaphore_signal(barrier, inc=1, device_id=(g, 1), device_id_type=MESH)

    for copy in tabs:
        copy.start()
    for r in range(1, groups):
        pl.semaphore_signal(barrier, inc=1, device_id=(lax.rem(g + r, groups), 0), device_id_type=MESH)

    def newell_row(part, p):
        t = (2 * g + part) * pairs + p
        return (1 - c) * t + c * lax.rem(rows - t, rows)

    near = [
        pltpu.make_async_copy(newell.at[newell_row(c, p)], nwl.at[c, p], near_sem.at[0]) for p in range(pairs)
    ]

    @pl.when(c == 1)
    def _():
        pl.semaphore_wait(barrier, 1)
        pl.semaphore_signal(hand.at[0], inc=1, device_id=(g, 0), device_id_type=MESH)

    @pl.when(c == 0)
    def _():
        pl.semaphore_wait(hand.at[0], 1)

    swap = [
        pltpu.make_async_remote_copy(
            src_ref=mag.at[0, comp],
            dst_ref=mag.at[1, comp],
            send_sem=pair_sem.at[0],
            recv_sem=swap_recv.at[comp],
            device_id=(g, other),
            device_id_type=MESH,
        )
        for comp in range(3)
    ]
    for comp in range(3):
        loads[comp].wait()
        swap[comp].start()

    def far(p, count):
        at = pl.ds(p, count)
        row = newell_row(other, p)
        return pltpu.make_async_remote_copy(
            src_ref=newell.at[pl.ds(row, 1)] if count == 1 else nwl.at[c, at],
            dst_ref=nwl.at[c, at],
            send_sem=pair_sem.at[1],
            recv_sem=pair_sem.at[2],
            device_id=(g, other),
            device_id_type=MESH,
        )

    for copy in near + late:
        copy.start()
    for p in range(pairs):
        far(p, 1).start()

    for copy in tabs:
        copy.wait()
    def along_z(side, comp):
        return jnp.dot(mag[side, comp], zf[...], preferred_element_type=F32).astype(BF16)

    for comp in range(3):
        zrow[pl.ds(0, rows), pl.ds(2 * comp * half, 2 * half)] = along_z(0, comp)
    own_part = True
    if own_part:
        spec[...] = jnp.dot(yf[:, :rows], zrow[pl.ds(0, rows), :], preferred_element_type=F32)
    for comp in range(3):
        at = pl.ds(2 * comp * half, 2 * half)
        swap[comp].wait_recv()
        far_rows = along_z(1, comp)
        if own_part:
            part = spec[:, at] + jnp.dot(yf[:, rows:], far_rows, preferred_element_type=F32)
        else:
            zrow[pl.ds(rows, rows), at] = far_rows
            part = jnp.dot(yf[...], zrow[:, at], preferred_element_type=F32)
        if whole_tiles:
            for i in range(groups):
                send[i, :, at] = part[i * own : (i + 1) * own].astype(BF16)
        else:
            spec[:, at] = part
    if not whole_tiles:
        for i in range(groups):
            send[i] = spec[pl.ds(i * own, own), :].astype(BF16)

    @pl.when(c == 0)
    def _():
        pl.semaphore_wait(barrier, 2 * (groups - 1))
        pl.semaphore_signal(hand.at[1], inc=1, device_id=(g, 1), device_id_type=MESH)

    @pl.when(c == 1)
    def _():
        pl.semaphore_wait(hand.at[1], 1)

    def forward(to):
        return pltpu.make_async_remote_copy(
            src_ref=send.at[to],
            dst_ref=recv.at[g],
            send_sem=fwd_send.at[0],
            recv_sem=fwd_recv.at[my_layer],
            device_id=(to, c),
            device_id_type=MESH,
        )

    for k in range(1, groups):
        forward(target(k)).start()

    def waiter(ref, send_sem, recv_sem):
        return pltpu.make_async_remote_copy(
            src_ref=ref,
            dst_ref=ref,
            send_sem=send_sem,
            recv_sem=recv_sem,
            device_id=(g, other),
            device_id_type=MESH,
        )

    lane = lax.broadcasted_iota(jnp.int32, (own, half), 1)
    row = lax.broadcasted_iota(jnp.int32, (own, half), 0)
    top = row < pairs

    first_t = (2 * g + c) * pairs + lax.rem(row, pairs)
    al = first_t == 0
    ln = jnp.logical_and(lane == 0, first_t > 0)
    special, ln_low = jnp.logical_or(al, ln), jnp.logical_and(ln, jnp.logical_not(top))

    def flip(v):
        return jnp.concatenate([v[pairs:], v[:pairs]], axis=0)

    def wait_layer(layer):
        sem = fwd_recv.at[layer]

        @pl.when(layer == my_layer)
        def _():
            waiter(recv.at[pl.ds(0, plane - 1)], fwd_send.at[0], sem).wait_recv()

        @pl.when(layer != my_layer)
        def _():
            waiter(recv.at[pl.ds(0, plane)], fwd_send.at[0], sem).wait_recv()

    def unpack(j):
        block = recv[j].astype(F32)
        parts = []
        for comp in range(3):
            re = block[:, 2 * comp * half : (2 * comp + 1) * half]
            im = block[:, (2 * comp + 1) * half : (2 * comp + 2) * half]
            re_f, im_f = flip(re), flip(im)
            new_re = jnp.where(top, re + im_f, re_f - im)
            new_im = jnp.where(top, im - re_f, im_f + re)
            lone_re = jnp.where(ln_low, im_f, re)
            lone_im = jnp.where(al, im, -jnp.where(top, re_f, im))
            parts.append(jnp.where(special, lone_re, new_re))
            parts.append(jnp.where(special, lone_im, new_im))
        return parts

    def k_of(entry, d):
        start = pl.multiple_of((entry * cells + d) * own, own)
        return kern[pl.ds(start, own), :]

    def add_layer(layer, sources, i):
        total = [acc[i, q] for q in range(6)]
        for p in range(plane):
            j = layer * plane + p
            d = jnp.abs(i - j)
            signed = jnp.where(i >= j, 4, 10)
            xx, yy, zz, yz = (k_of(e, d) for e in range(4))
            xy, xz = k_of(signed, d), k_of(signed + 1, d)
            xxi, yyi, zzi, yzi = (k_of(6 + e, d) for e in range(4))
            xr, xi, yr, yim, zr, zim = sources[p]
            total[0] += xx * xr - xy * yim - xz * zim
            total[1] += xxi * xi + xy * yr + xz * zr
            total[2] += yy * yr + yz * zr - xy * xi
            total[3] += yyi * yim + yzi * zim + xy * xr
            total[4] += yz * yr + zz * zr - xz * xi
            total[5] += yzi * yim + zzi * zim + xz * xr
        return total

    def backward(i):
        return pltpu.make_async_remote_copy(
            src_ref=back.at[i],
            dst_ref=fields.at[c, g],
            send_sem=bwd_send.at[0],
            recv_sem=bwd_recv.at[my_layer],
            device_id=(i, c),
            device_id_type=MESH,
        )

    def prepare():
        recv[g] = send[g]
        for copy in near:
            copy.wait()
        far(0, pairs).wait_recv()
        late[0].wait()
        table_rows = 6 * cells
        even_rows = 4 * cells
        lane0 = lax.broadcasted_iota(jnp.int32, (table_rows, half), 1) == 0
        even = lax.broadcasted_iota(jnp.int32, (table_rows, half), 0) < even_rows
        sign = jnp.where(even, 1.0, -1.0).astype(F32)
        row_of = lax.broadcasted_iota(jnp.int32, (table_rows, half), 0)
        diagonal = functools.reduce(jnp.logical_or, [row_of == entry * cells + 1 for entry in range(3)])
        neighbour = jnp.where(diagonal, -2.0 * EXCHANGE, 0.0).astype(F32)
        for p in range(pairs):
            first = nwl[0, p].reshape(table_rows, 2 * half)
            mirror = nwl[1, p].reshape(table_rows, 2 * half)
            rev_first = jnp.dot(first, rv[...], preferred_element_type=F32)
            rev_mirror = jnp.dot(mirror, rv[...], preferred_element_type=F32)
            lo_first, hi_first = first[:, :half].astype(F32), first[:, half:].astype(F32)
            lo_mirror, hi_mirror = mirror[:, :half].astype(F32), mirror[:, half:].astype(F32)
            if p == 0:
                alone = ((2 * g + c) * pairs == 0).astype(F32)
                paired = 1.0 - alone
                of_first = alone * rev_first + paired * rev_mirror
                of_mirror = alone * rev_mirror + paired * rev_first
            else:
                of_first, of_mirror = rev_mirror, rev_first
            k_first = lo_first + sign * of_first
            k_mirror = lo_mirror + sign * of_mirror
            middle = hi_first + sign * hi_mirror
            if p == 0:
                i_first = jnp.where(lane0, alone * (2.0 * hi_first) + paired * k_first, k_first)
                i_mirror = jnp.where(lane0, alone * (2.0 * hi_mirror) + paired * middle, k_mirror)
                k_mirror = jnp.where(lane0, alone * k_mirror + paired * middle, k_mirror)
            else:
                k_mirror = jnp.where(lane0, middle, k_mirror)
                i_first, i_mirror = k_first, k_mirror
            for place, k_all, i_all in ((p, k_first, i_first), (pairs + p, k_mirror, i_mirror)):
                k_all, i_all = k_all + neighbour, i_all + neighbour
                kern[pl.ds(place, table_rows, stride=own), :] = k_all
                kern[pl.ds(table_rows * own + place, even_rows, stride=own), :] = i_all[:even_rows]
                kern[pl.ds((table_rows + even_rows) * own + place, 2 * cells, stride=own), :] = -k_all[even_rows:]
        acc[...] = jnp.zeros(acc.shape, F32)

    def gather(layer):
        wait_layer(layer)
        sources = [unpack(layer * plane + p) for p in range(plane)]

        def over(n, inner):
            for p in range(plane):
                i = n * plane + p
                total = add_layer(layer, sources, i)
                for q in range(6):
                    acc[i, q] = total[q]
            return inner

        lax.fori_loop(0, layers, over, 0)

    def finish(layer):
        wait_layer(layer)
        sources = [unpack(layer * plane + p) for p in range(plane)]

        def dispatch(n):
            for p in range(plane):
                i = target(n * plane + p)

                @pl.when(i != g)
                def _():
                    backward(i).start()

        def over(n, carry):
            for p in range(plane):
                i = target(n * plane + p)
                spread(i, add_layer(layer, sources, i))

            @pl.when(n > 0)
            def _():
                dispatch(jnp.maximum(n - 1, 0))

            return carry

        def spread(i, total):
            for comp in range(3):
                re, im = total[2 * comp], total[2 * comp + 1]
                re_f, im_f = flip(re), flip(im)
                new_re = jnp.where(top, re + re_f, im - im_f)
                new_im = jnp.where(top, im + im_f, re_f - re)
                lone_re = jnp.where(al, re, 2.0 * jnp.where(top, re, -im_f))
                lone_im = jnp.where(al, im, 2.0 * jnp.where(top, re_f, -im))
                new_re = jnp.where(special, lone_re, new_re)
                new_im = jnp.where(special, lone_im, new_im)
                back[i, :, pl.ds(2 * comp * half, half)] = new_re.astype(BF16)
                back[i, :, pl.ds((2 * comp + 1) * half, half)] = new_im.astype(BF16)

        lax.fori_loop(0, layers, over, 0)
        dispatch(layers - 1)
        fields[c, g] = back[g]

    prepare()
    beside = (g > 0).astype(F32) + (g < groups - 1).astype(F32)
    for comp in range(3):
        full = jnp.concatenate([mag[0, comp], mag[1, comp]], axis=0).astype(F32)
        centre = full[:rows]
        total = pltpu.roll(full, 1, 0)[:rows] + pltpu.roll(full, 2 * rows - 1, 0)[:rows]
        total = total + pltpu.roll(centre, 1, 1) + pltpu.roll(centre, 2 * half - 1, 1)
        lap[comp] = EXCHANGE * (total - (4.0 + beside) * centre)

    def step(t, carry):
        gather(group_at(t))
        return carry

    lax.fori_loop(0, layers - 1, step, 0)
    finish(group_at(layers - 1))

    def relay(n):
        return pltpu.make_async_remote_copy(
            src_ref=fields.at[c, pl.ds(n * plane, plane)],
            dst_ref=fields.at[c, pl.ds(n * plane, plane)],
            send_sem=rel_sem.at[0],
            recv_sem=rel_sem.at[1],
            device_id=(g, other),
            device_id_type=MESH,
        )

    for k in range(layers):
        n = relay_at(k)

        @pl.when(n == my_layer)
        def _():
            waiter(fields.at[c, pl.ds(0, plane - 1)], bwd_send.at[0], bwd_recv.at[n]).wait_recv()

        @pl.when(n != my_layer)
        def _():
            waiter(fields.at[c, pl.ds(0, plane)], bwd_send.at[0], bwd_recv.at[n]).wait_recv()

        relay(n).start()

    for copy in late[1:]:
        copy.wait()
    waiter(fields.at[other], rel_sem.at[0], rel_sem.at[1]).wait_recv()

    if whole_tiles:
        modes = fields[...].reshape(2 * groups * own, wide)
    else:
        for part in range(2):
            for i in range(groups):
                stack[pl.ds((part * groups + i) * own, own), :] = fields[part, i].astype(F32)
        modes = stack[...].astype(BF16)
    scale = 1.0 / (2 * rows * 2 * half)
    for comp in range(3):
        at = slice(2 * comp * half, 2 * (comp + 1) * half)
        g_rows = jnp.dot(yi[...], modes[:, at], preferred_element_type=F32).astype(BF16)
        demag = jnp.dot(g_rows, zi[...], preferred_element_type=F32) * scale
        out[comp] = (demag + lap[comp]).astype(BF16)

    waiter(mag.at[0], pair_sem.at[0], swap_recv.at[0]).wait_send()
    waiter(fields.at[c], rel_sem.at[0], rel_sem.at[1]).wait_send()
    far(0, pairs).wait_send()
    waiter(back.at[pl.ds(0, groups - 1)], bwd_send.at[0], bwd_recv.at[0]).wait_send()
    waiter(send.at[pl.ds(0, groups - 1)], fwd_send.at[0], fwd_recv.at[0]).wait_send()


def on_device(magnet, newell, *consts):
    rows, _, x_cells, z_total = magnet.shape
    groups = lax.axis_size("gx")
    parts = lax.axis_size("yz")
    assert x_cells == 1 and parts == 2
    y_total = rows * parts
    pairs = y_total // (groups * parts * 2)
    own = 2 * pairs
    half = z_total // 2
    wide = 3 * z_total
    layers = groups // math.gcd(groups, 4)
    any_ref = pl.BlockSpec(memory_space=pl.ANY)
    dma = pltpu.SemaphoreType.DMA
    planes = jnp.transpose(magnet[:, :, 0, :], (1, 0, 2))
    field = pl.pallas_call(
        functools.partial(kernel, groups, pairs),
        out_shape=pltpu.VMEM(planes.shape, BF16),
        in_specs=[any_ref] * 7,
        out_specs=pl.BlockSpec(memory_space=pltpu.VMEM),
        scratch_shapes=[
            pltpu.VMEM((2, 3, rows, z_total), BF16),
            pltpu.VMEM((2, pairs, 6, groups, z_total), BF16),
            pltpu.VMEM((rows, y_total), BF16),
            pltpu.VMEM((rows, y_total), BF16),
            pltpu.VMEM((z_total, z_total), BF16),
            pltpu.VMEM((z_total, z_total), BF16),
            pltpu.VMEM((z_total, half), BF16),
            pltpu.VMEM((y_total, wide), BF16),
            pltpu.VMEM((rows, wide), F32),
            pltpu.VMEM((groups, own, wide), BF16),
            pltpu.VMEM((groups, own, wide), BF16),
            pltpu.VMEM((12 * groups * own, half), F32),
            pltpu.VMEM((groups, 6, own, half), F32),
            pltpu.VMEM((groups, own, wide), BF16),
            pltpu.VMEM((2, groups, own, wide), BF16),
            pltpu.VMEM((y_total, wide), F32),
            pltpu.VMEM((3, rows, z_total), F32),
            dma((8,)),
            dma((1,)),
            dma((3,)),
            dma((3,)),
            dma((1,)),
            dma((layers,)),
            dma((1,)),
            dma((layers,)),
            dma((2,)),
            pltpu.SemaphoreType.REGULAR((2,)),
        ],
        compiler_params=pltpu.CompilerParams(collective_id=0, has_side_effects=True),
    )(planes, newell, *consts)
    return jnp.transpose(field, (1, 0, 2))[:, :, None, :]


def solution(mesh):
    groups, parts = mesh.shape["gx"], mesh.shape["yz"]

    def run(magnet, newell):
        consts = tables(groups, parts, magnet.shape[0], magnet.shape[3])
        body = lambda m, n: on_device(m, n, *[jnp.asarray(t) for t in consts])
        return jax.shard_map(
            body,
            mesh=mesh,
            in_specs=(P("yz", None, "gx", None), P("yz", None, None, None)),
            out_specs=P("yz", None, "gx", None),
            check_vma=False,
        )(magnet, newell)

    return run
```

time: 23 us -> 21.9 us (0.952)
  Pallas kernels: 21.8 us -> 20.9 us
    pallas_call x1, Pallas kernels: 21.8 us -> 20.9 us  [on_device(): pl.pallas_call(functools.partial(kernel, groups, pairs), out_shape=pltpu....]
where the time goes in v3:
time: 21.9 us; the launch traced here: 21.6 us
  Pallas kernels  20.9 us (95%)
  local copies, waits for them, and re-layouts  0.68 us (3%)
    pallas_call x1, Pallas kernels, on_device(): pl.pallas_call(functools.partial(kernel, groups, pairs), out_shape=pltpu....  20.9 us
    unnamed x1, local copies, waits for them, and re-layouts  0.68 us

profile of v3, /device:TPU:0, one launch (start us, length us, event | category | flops | bytes accessed | tf_op | source)
XLA Modules:
  0.0 21.6 jit_solution(3247353031108065135)
XLA Ops:
  0.0 20.9 %shard_map.73 = bf16[3,128,256]{2,1,0:T(8,128)(2,1)S(1)} custom-call(bf16[3,128,256]{2,1,0:T(8,128)(2,1)} %bitcast.9, bf16[128,6,16,256]{3,2,1,0:T(8,128)(2,1)} %newell.1, bf16[2,128,256]{2,1,0:T(8,128)(2,1)} %constant.10.clone.y_fwd, bf16[2,128,256]{2,1,0:T(8,128)(2,1)} %constant.11.clone.y_inv, bf16[256,256]{1,0:T(8,128)(2,1)} %constant.12.clone.z_fwd, ...), custom_call_target="tpu_custom_call" | custom-call | tf_op jit(solution)/shard_map/pallas_call | solution.py:474
  20.9 0.7 %copy.10 = bf16[128,3,1,256]{3,0,2,1:T(8,128)(2,1)} copy(bf16[128,3,1,256]{3,0,2,1:T(8,128)(2,1)S(1)} %bitcast.8) | data formatting | bytes 393216

commit v4 on v3

--- a/solution.py
+++ b/solution.py
@@ -74,6 +74,12 @@
     whole_tiles = own % 8 == 0
 
     my_layer = g // plane
+
+    def is_late(b):
+        return b // plane + lax.rem(b, plane) // 2 + lax.rem(b, 2) >= layers + 1
+
+    late_count = sum(int(b // plane + b % plane // 2 + b % 2 >= layers + 1) for b in range(groups))
+    lower = g < groups // 2
     low = 2 * my_layer < layers
     from_edge = jnp.where(low, my_layer, layers - 1 - my_layer)
 
@@ -84,11 +90,15 @@
     def target(k):
         return lax.rem(g + k, groups)
 
+    def target_back(k):
+        zero_at = lax.rem(groups - g, groups)
+        return jnp.where(k == 0, 0, jnp.where(k <= zero_at, target(jnp.maximum(k - 1, 0)), target(k)))
+
+    def group_at(t):
+        return lax.rem(my_layer + layers - t, layers)
+
     def relay_at(t):
         return layer_at(t)
-
-    def group_at(t):
-        return lax.rem(my_layer + layers - t, layers)
 
     barrier = pltpu.get_barrier_semaphore()
     loads = [
@@ -113,7 +123,11 @@
     for copy in tabs:
         copy.start()
     for r in range(1, groups):
-        pl.semaphore_signal(barrier, inc=1, device_id=(lax.rem(g + r, groups), 0), device_id_type=MESH)
+        to = lax.rem(g + r, groups)
+
+        @pl.when(jnp.logical_or(jnp.logical_not(is_late(g)), to >= groups // 2))
+        def _():
+            pl.semaphore_signal(barrier, inc=1, device_id=(to, 0), device_id_type=MESH)
 
     def newell_row(part, p):
         t = (2 * g + part) * pairs + p
@@ -171,18 +185,12 @@
 
     for comp in range(3):
         zrow[pl.ds(0, rows), pl.ds(2 * comp * half, 2 * half)] = along_z(0, comp)
-    own_part = True
-    if own_part:
-        spec[...] = jnp.dot(yf[:, :rows], zrow[pl.ds(0, rows), :], preferred_element_type=F32)
+    spec[...] = jnp.dot(yf[:, :rows], zrow[pl.ds(0, rows), :], preferred_element_type=F32)
+    for copy in swap:
+        copy.wait_recv()
     for comp in range(3):
         at = pl.ds(2 * comp * half, 2 * half)
-        swap[comp].wait_recv()
-        far_rows = along_z(1, comp)
-        if own_part:
-            part = spec[:, at] + jnp.dot(yf[:, rows:], far_rows, preferred_element_type=F32)
-        else:
-            zrow[pl.ds(rows, rows), at] = far_rows
-            part = jnp.dot(yf[...], zrow[:, at], preferred_element_type=F32)
+        part = spec[:, at] + jnp.dot(yf[:, rows:], along_z(1, comp), preferred_element_type=F32)
         if whole_tiles:
             for i in range(groups):
                 send[i, :, at] = part[i * own : (i + 1) * own].astype(BF16)
@@ -194,8 +202,14 @@
 
     @pl.when(c == 0)
     def _():
-        pl.semaphore_wait(barrier, 2 * (groups - 1))
+        pl.semaphore_wait(barrier, 2 * (groups - 1 - late_count * lower.astype(jnp.int32)))
         pl.semaphore_signal(hand.at[1], inc=1, device_id=(g, 1), device_id_type=MESH)
+
+        @pl.when(is_late(g))
+        def _():
+            for to in range(groups // 2):
+                for core in range(2):
+                    pl.semaphore_signal(hand.at[2], inc=1, device_id=(to, core), device_id_type=MESH)
 
     @pl.when(c == 1)
     def _():
@@ -212,7 +226,11 @@
         )
 
     for k in range(1, groups):
-        forward(target(k)).start()
+        to = target(k)
+
+        @pl.when(jnp.logical_not(jnp.logical_and(lower, is_late(to))))
+        def _():
+            forward(to).start()
 
     def waiter(ref, send_sem, recv_sem):
         return pltpu.make_async_remote_copy(
@@ -289,8 +307,8 @@
             src_ref=back.at[i],
             dst_ref=fields.at[c, g],
             send_sem=bwd_send.at[0],
-            recv_sem=bwd_recv.at[my_layer],
-            device_id=(i, c),
+            recv_sem=bwd_recv.at[c * layers + my_layer],
+            device_id=(i, 1),
             device_id_type=MESH,
         )
 
@@ -357,17 +375,19 @@
         wait_layer(layer)
         sources = [unpack(layer * plane + p) for p in range(plane)]
 
+        chunk = 1
+
         def dispatch(n):
-            for p in range(plane):
-                i = target(n * plane + p)
+            for p in range(chunk):
+                i = target_back(n * chunk + p)
 
                 @pl.when(i != g)
                 def _():
                     backward(i).start()
 
         def over(n, carry):
-            for p in range(plane):
-                i = target(n * plane + p)
+            for p in range(chunk):
+                i = target_back(n * chunk + p)
                 spread(i, add_layer(layer, sources, i))
 
             @pl.when(n > 0)
@@ -389,9 +409,12 @@
                 back[i, :, pl.ds(2 * comp * half, half)] = new_re.astype(BF16)
                 back[i, :, pl.ds((2 * comp + 1) * half, half)] = new_im.astype(BF16)
 
-        lax.fori_loop(0, layers, over, 0)
-        dispatch(layers - 1)
-        fields[c, g] = back[g]
+        lax.fori_loop(0, groups // chunk, over, 0)
+        dispatch(groups // chunk - 1)
+
+        @pl.when(c == 1)
+        def _():
+            fields[1, g] = back[g]
 
     prepare()
     beside = (g > 0).astype(F32) + (g < groups - 1).astype(F32)
@@ -402,6 +425,17 @@
         total = total + pltpu.roll(centre, 1, 1) + pltpu.roll(centre, 2 * half - 1, 1)
         lap[comp] = EXCHANGE * (total - (4.0 + beside) * centre)
 
+    if late_count:
+        @pl.when(lower)
+        def _():
+            pl.semaphore_wait(hand.at[2], late_count)
+            for k in range(1, groups):
+                to = target(k)
+
+                @pl.when(is_late(to))
+                def _():
+                    forward(to).start()
+
     def step(t, carry):
         gather(group_at(t))
         return carry
@@ -409,32 +443,51 @@
     lax.fori_loop(0, layers - 1, step, 0)
     finish(group_at(layers - 1))
 
-    def relay(n):
+    for copy in late[1:]:
+        copy.wait()
+
+    def relay(part, n):
+        at = pl.ds(n * plane, plane)
         return pltpu.make_async_remote_copy(
-            src_ref=fields.at[c, pl.ds(n * plane, plane)],
-            dst_ref=fields.at[c, pl.ds(n * plane, plane)],
+            src_ref=fields.at[part, at],
+            dst_ref=fields.at[part, at],
             send_sem=rel_sem.at[0],
             recv_sem=rel_sem.at[1],
-            device_id=(g, other),
+            device_id=(g, 0),
             device_id_type=MESH,
         )
 
-    for k in range(layers):
-        n = relay_at(k)
-
-        @pl.when(n == my_layer)
-        def _():
-            waiter(fields.at[c, pl.ds(0, plane - 1)], bwd_send.at[0], bwd_recv.at[n]).wait_recv()
-
-        @pl.when(n != my_layer)
-        def _():
-            waiter(fields.at[c, pl.ds(0, plane)], bwd_send.at[0], bwd_recv.at[n]).wait_recv()
-
-        relay(n).start()
-
-    for copy in late[1:]:
-        copy.wait()
-    waiter(fields.at[other], rel_sem.at[0], rel_sem.at[1]).wait_recv()
+    own_block = pltpu.make_async_remote_copy(
+        src_ref=back.at[g],
+        dst_ref=fields.at[0, g],
+        send_sem=bwd_send.at[0],
+        recv_sem=bwd_recv.at[my_layer],
+        device_id=(g, 1),
+        device_id_type=MESH,
+    )
+
+    @pl.when(c == 0)
+    def _():
+        own_block.start()
+        waiter(fields, rel_sem.at[0], rel_sem.at[1]).wait_recv()
+
+    @pl.when(c == 1)
+    def _():
+        for k in range(layers):
+            n = relay_at(k)
+            for part in (1, 0):
+                sem = bwd_recv.at[part * layers + n]
+                if part == 1:
+                    @pl.when(n == my_layer)
+                    def _():
+                        waiter(fields.at[1, pl.ds(0, plane - 1)], bwd_send.at[0], sem).wait_recv()
+
+                    @pl.when(n != my_layer)
+                    def _():
+                        waiter(fields.at[1, pl.ds(0, plane)], bwd_send.at[0], sem).wait_recv()
+                else:
+                    waiter(fields.at[0, pl.ds(0, plane)], bwd_send.at[0], sem).wait_recv()
+                relay(part, n).start()
 
     if whole_tiles:
         modes = fields[...].reshape(2 * groups * own, wide)
@@ -451,7 +504,15 @@
         out[comp] = (demag + lap[comp]).astype(BF16)
 
     waiter(mag.at[0], pair_sem.at[0], swap_recv.at[0]).wait_send()
-    waiter(fields.at[c], rel_sem.at[0], rel_sem.at[1]).wait_send()
+
+    @pl.when(c == 0)
+    def _():
+        own_block.wait_send()
+
+    @pl.when(c == 1)
+    def _():
+        waiter(fields, rel_sem.at[0], rel_sem.at[1]).wait_send()
+
     far(0, pairs).wait_send()
     waiter(back.at[pl.ds(0, groups - 1)], bwd_send.at[0], bwd_recv.at[0]).wait_send()
     waiter(send.at[pl.ds(0, groups - 1)], fwd_send.at[0], fwd_recv.at[0]).wait_send()
@@ -501,9 +562,9 @@
             dma((1,)),
             dma((layers,)),
             dma((1,)),
-            dma((layers,)),
+            dma((2 * layers,)),
             dma((2,)),
-            pltpu.SemaphoreType.REGULAR((2,)),
+            pltpu.SemaphoreType.REGULAR((3,)),
         ],
         compiler_params=pltpu.CompilerParams(collective_id=0, has_side_effects=True),
     )(planes, newell, *consts)

time: 21.9 us -> 21.2 us (0.968)
  Pallas kernels: 20.9 us -> 20.3 us
    pallas_call x1, Pallas kernels: 20.9 us -> 20.3 us  [on_device(): pl.pallas_call(functools.partial(kernel, groups, pairs), out_shape=pltpu....]
where the time goes in v4:
time: 21.2 us; the launch traced here: 21 us
  Pallas kernels  20.3 us (96%)
  local copies, waits for them, and re-layouts  0.68 us (3%)
    pallas_call x1, Pallas kernels, on_device(): pl.pallas_call(functools.partial(kernel, groups, pairs), out_shape=pltpu....  20.3 us
    unnamed x1, local copies, waits for them, and re-layouts  0.68 us

profile of v4, /device:TPU:0, one launch (start us, length us, event | category | flops | bytes accessed | tf_op | source)
XLA Modules:
  0.0 21.0 jit_solution(9189602044011553608)
XLA Ops:
  0.0 20.3 %shard_map.73 = bf16[3,128,256]{2,1,0:T(8,128)(2,1)S(1)} custom-call(bf16[3,128,256]{2,1,0:T(8,128)(2,1)} %bitcast.9, bf16[128,6,16,256]{3,2,1,0:T(8,128)(2,1)} %newell.1, bf16[2,128,256]{2,1,0:T(8,128)(2,1)} %constant.10.clone.y_fwd, bf16[2,128,256]{2,1,0:T(8,128)(2,1)} %constant.11.clone.y_inv, bf16[256,256]{1,0:T(8,128)(2,1)} %constant.12.clone.z_fwd, ...), custom_call_target="tpu_custom_call" | custom-call | tf_op jit(solution)/shard_map/pallas_call | solution.py:535
  20.3 0.7 %copy.10 = bf16[128,3,1,256]{3,0,2,1:T(8,128)(2,1)} copy(bf16[128,3,1,256]{3,0,2,1:T(8,128)(2,1)S(1)} %bitcast.8) | data formatting | bytes 393216

commit v5 on v4

--- a/solution.py
+++ b/solution.py
@@ -178,6 +178,23 @@
     for p in range(pairs):
         far(p, 1).start()
 
+    def meet():
+        @pl.when(c == 0)
+        def _():
+            pl.semaphore_wait(barrier, 2 * (groups - 1 - late_count * lower.astype(jnp.int32)))
+
+            @pl.when(is_late(g))
+            def _():
+                for to in range(groups // 2):
+                    for core in range(2):
+                        pl.semaphore_signal(hand.at[2], inc=1, device_id=(to, core), device_id_type=MESH)
+
+            pl.semaphore_signal(hand.at[1], inc=1, device_id=(g, 1), device_id_type=MESH)
+
+        @pl.when(c == 1)
+        def _():
+            pl.semaphore_wait(hand.at[1], 1)
+
     for copy in tabs:
         copy.wait()
     def along_z(side, comp):
@@ -186,6 +203,10 @@
     for comp in range(3):
         zrow[pl.ds(0, rows), pl.ds(2 * comp * half, 2 * half)] = along_z(0, comp)
     spec[...] = jnp.dot(yf[:, :rows], zrow[pl.ds(0, rows), :], preferred_element_type=F32)
+    @pl.when(is_late(g))
+    def _():
+        meet()
+
     for copy in swap:
         copy.wait_recv()
     for comp in range(3):
@@ -200,20 +221,9 @@
         for i in range(groups):
             send[i] = spec[pl.ds(i * own, own), :].astype(BF16)
 
-    @pl.when(c == 0)
-    def _():
-        pl.semaphore_wait(barrier, 2 * (groups - 1 - late_count * lower.astype(jnp.int32)))
-        pl.semaphore_signal(hand.at[1], inc=1, device_id=(g, 1), device_id_type=MESH)
-
-        @pl.when(is_late(g))
-        def _():
-            for to in range(groups // 2):
-                for core in range(2):
-                    pl.semaphore_signal(hand.at[2], inc=1, device_id=(to, core), device_id_type=MESH)
-
-    @pl.when(c == 1)
-    def _():
-        pl.semaphore_wait(hand.at[1], 1)
+    @pl.when(jnp.logical_not(is_late(g)))
+    def _():
+        meet()
 
     def forward(to):
         return pltpu.make_async_remote_copy(
@@ -302,15 +312,18 @@
             total[5] += yzi * yim + zzi * zim + xz * xr
         return total
 
-    def backward(i):
+    def backward(i, core=1):
         return pltpu.make_async_remote_copy(
             src_ref=back.at[i],
             dst_ref=fields.at[c, g],
             send_sem=bwd_send.at[0],
             recv_sem=bwd_recv.at[c * layers + my_layer],
-            device_id=(i, 1),
+            device_id=(i, core),
             device_id_type=MESH,
         )
+
+    direct = layers - 1
+    twice = jnp.logical_and(c == 0, my_layer == direct)
 
     def prepare():
         recv[g] = send[g]
@@ -375,20 +388,21 @@
         wait_layer(layer)
         sources = [unpack(layer * plane + p) for p in range(plane)]
 
-        chunk = 1
 
         def dispatch(n):
-            for p in range(chunk):
-                i = target_back(n * chunk + p)
-
-                @pl.when(i != g)
-                def _():
-                    backward(i).start()
+            i = target_back(n)
+
+            @pl.when(i != g)
+            def _():
+                backward(i).start()
+
+            @pl.when(jnp.logical_and(i == 0, twice))
+            def _():
+                backward(i, 0).start()
 
         def over(n, carry):
-            for p in range(chunk):
-                i = target_back(n * chunk + p)
-                spread(i, add_layer(layer, sources, i))
+            i = target_back(n)
+            spread(i, add_layer(layer, sources, i))
 
             @pl.when(n > 0)
             def _():
@@ -409,8 +423,8 @@
                 back[i, :, pl.ds(2 * comp * half, half)] = new_re.astype(BF16)
                 back[i, :, pl.ds((2 * comp + 1) * half, half)] = new_im.astype(BF16)
 
-        lax.fori_loop(0, groups // chunk, over, 0)
-        dispatch(groups // chunk - 1)
+        lax.fori_loop(0, groups, over, 0)
+        dispatch(groups - 1)
 
         @pl.when(c == 1)
         def _():
@@ -469,7 +483,16 @@
     @pl.when(c == 0)
     def _():
         own_block.start()
-        waiter(fields, rel_sem.at[0], rel_sem.at[1]).wait_recv()
+
+        @pl.when(g == 0)
+        def _():
+            waiter(fields.at[:, pl.ds(0, groups - plane // 2)], rel_sem.at[0], rel_sem.at[1]).wait_recv()
+            at = pl.ds(direct * plane, plane)
+            waiter(fields.at[0, at], bwd_send.at[0], bwd_recv.at[direct]).wait_recv()
+
+        @pl.when(g != 0)
+        def _():
+            waiter(fields, rel_sem.at[0], rel_sem.at[1]).wait_recv()
 
     @pl.when(c == 1)
     def _():
@@ -487,7 +510,12 @@
                         waiter(fields.at[1, pl.ds(0, plane)], bwd_send.at[0], sem).wait_recv()
                 else:
                     waiter(fields.at[0, pl.ds(0, plane)], bwd_send.at[0], sem).wait_recv()
-                relay(part, n).start()
+                if part == 1:
+                    relay(part, n).start()
+                else:
+                    @pl.when(jnp.logical_or(g != 0, n != direct))
+                    def _():
+                        relay(part, n).start()
 
     if whole_tiles:
         modes = fields[...].reshape(2 * groups * own, wide)
@@ -509,9 +537,19 @@
     def _():
         own_block.wait_send()
 
+    @pl.when(twice)
+    def _():
+        backward(0, 0).wait_send()
+
     @pl.when(c == 1)
     def _():
-        waiter(fields, rel_sem.at[0], rel_sem.at[1]).wait_send()
+        @pl.when(g == 0)
+        def _():
+            waiter(fields.at[:, pl.ds(0, groups - plane // 2)], rel_sem.at[0], rel_sem.at[1]).wait_send()
+
+        @pl.when(g != 0)
+        def _():
+            waiter(fields, rel_sem.at[0], rel_sem.at[1]).wait_send()
 
     far(0, pairs).wait_send()
     waiter(back.at[pl.ds(0, groups - 1)], bwd_send.at[0], bwd_recv.at[0]).wait_send()

time: 21.2 us -> 20.5 us (0.967)
  Pallas kernels: 20.3 us -> 19.7 us
    pallas_call x1, Pallas kernels: 20.3 us -> 19.7 us  [on_device(): pl.pallas_call(functools.partial(kernel, groups, pairs), out_shape=pltpu....]
where the time goes in v5:
time: 20.5 us; the launch traced here: 20.4 us
  Pallas kernels  19.7 us (96%)
  local copies, waits for them, and re-layouts  0.68 us (3%)
    pallas_call x1, Pallas kernels, on_device(): pl.pallas_call(functools.partial(kernel, groups, pairs), out_shape=pltpu....  19.7 us
    unnamed x1, local copies, waits for them, and re-layouts  0.68 us

profile of v5, /device:TPU:0, one launch (start us, length us, event | category | flops | bytes accessed | tf_op | source)
XLA Modules:
  0.0 20.4 jit_solution(4664265581450142428)
XLA Ops:
  0.0 19.7 %shard_map.73 = bf16[3,128,256]{2,1,0:T(8,128)(2,1)S(1)} custom-call(bf16[3,128,256]{2,1,0:T(8,128)(2,1)} %bitcast.9, bf16[128,6,16,256]{3,2,1,0:T(8,128)(2,1)} %newell.1, bf16[2,128,256]{2,1,0:T(8,128)(2,1)} %constant.10.clone.y_fwd, bf16[2,128,256]{2,1,0:T(8,128)(2,1)} %constant.11.clone.y_inv, bf16[256,256]{1,0:T(8,128)(2,1)} %constant.12.clone.z_fwd, ...), custom_call_target="tpu_custom_call" | custom-call | tf_op jit(solution)/shard_map/pallas_call | solution.py:573
  19.7 0.7 %copy.10 = bf16[128,3,1,256]{3,0,2,1:T(8,128)(2,1)} copy(bf16[128,3,1,256]{3,0,2,1:T(8,128)(2,1)S(1)} %bitcast.8) | data formatting | bytes 393216

commit v6 on v5

--- a/solution.py
+++ b/solution.py
@@ -98,20 +98,20 @@
         return lax.rem(my_layer + layers - t, layers)
 
     def relay_at(t):
-        return layer_at(t)
+        return jnp.where(jnp.logical_and(my_layer == layers - 1, t >= 2), t - 2, jnp.where(t <= my_layer, my_layer - t, t))
 
     barrier = pltpu.get_barrier_semaphore()
     loads = [
-        pltpu.make_async_copy(magnet.at[comp], mag.at[0, comp], load_sem.at[comp]) for comp in range(3)
+        pltpu.make_async_copy(magnet.at[comp], mag.at[0, comp], load_sem.at[0]) for comp in range(3)
     ]
     tabs = [
-        pltpu.make_async_copy(z_fwd, zf, load_sem.at[3]),
-        pltpu.make_async_copy(y_fwd.at[c], yf, load_sem.at[4]),
+        pltpu.make_async_copy(z_fwd, zf, load_sem.at[1]),
+        pltpu.make_async_copy(y_fwd.at[c], yf, load_sem.at[2]),
     ]
     late = [
-        pltpu.make_async_copy(rev, rv, load_sem.at[5]),
-        pltpu.make_async_copy(y_inv.at[c], yi, load_sem.at[6]),
-        pltpu.make_async_copy(z_inv, zi, load_sem.at[7]),
+        pltpu.make_async_copy(rev, rv, load_sem.at[3]),
+        pltpu.make_async_copy(y_inv.at[c], yi, load_sem.at[4]),
+        pltpu.make_async_copy(z_inv, zi, load_sem.at[5]),
     ]
     for copy in loads:
         copy.start()
@@ -137,6 +137,16 @@
         pltpu.make_async_copy(newell.at[newell_row(c, p)], nwl.at[c, p], near_sem.at[0]) for p in range(pairs)
     ]
 
+    def waiter(ref, send_sem, recv_sem):
+        return pltpu.make_async_remote_copy(
+            src_ref=ref,
+            dst_ref=ref,
+            send_sem=send_sem,
+            recv_sem=recv_sem,
+            device_id=(g, other),
+            device_id_type=MESH,
+        )
+
     @pl.when(c == 1)
     def _():
         pl.semaphore_wait(barrier, 1)
@@ -145,21 +155,42 @@
     @pl.when(c == 0)
     def _():
         pl.semaphore_wait(hand.at[0], 1)
+
+    def meet():
+        @pl.when(c == 0)
+        def _():
+            pl.semaphore_wait(barrier, 2 * (groups - 1 - late_count * lower.astype(jnp.int32)))
+
+            @pl.when(is_late(g))
+            def _():
+                for to in range(groups // 2):
+                    for core in range(2):
+                        pl.semaphore_signal(hand.at[2], inc=1, device_id=(to, core), device_id_type=MESH)
+
+            pl.semaphore_signal(hand.at[1], inc=1, device_id=(g, 1), device_id_type=MESH)
+
+        @pl.when(c == 1)
+        def _():
+            pl.semaphore_wait(hand.at[1], 1)
+
+    @pl.when(is_late(g))
+    def _():
+        meet()
 
     swap = [
         pltpu.make_async_remote_copy(
             src_ref=mag.at[0, comp],
             dst_ref=mag.at[1, comp],
             send_sem=pair_sem.at[0],
-            recv_sem=swap_recv.at[comp],
+            recv_sem=swap_recv.at[0],
             device_id=(g, other),
             device_id_type=MESH,
         )
         for comp in range(3)
     ]
-    for comp in range(3):
-        loads[comp].wait()
-        swap[comp].start()
+    pltpu.make_async_copy(mag.at[0], mag.at[0], load_sem.at[0]).wait()
+    for copy in swap:
+        copy.start()
 
     def far(p, count):
         at = pl.ds(p, count)
@@ -178,23 +209,6 @@
     for p in range(pairs):
         far(p, 1).start()
 
-    def meet():
-        @pl.when(c == 0)
-        def _():
-            pl.semaphore_wait(barrier, 2 * (groups - 1 - late_count * lower.astype(jnp.int32)))
-
-            @pl.when(is_late(g))
-            def _():
-                for to in range(groups // 2):
-                    for core in range(2):
-                        pl.semaphore_signal(hand.at[2], inc=1, device_id=(to, core), device_id_type=MESH)
-
-            pl.semaphore_signal(hand.at[1], inc=1, device_id=(g, 1), device_id_type=MESH)
-
-        @pl.when(c == 1)
-        def _():
-            pl.semaphore_wait(hand.at[1], 1)
-
     for copy in tabs:
         copy.wait()
     def along_z(side, comp):
@@ -203,12 +217,7 @@
     for comp in range(3):
         zrow[pl.ds(0, rows), pl.ds(2 * comp * half, 2 * half)] = along_z(0, comp)
     spec[...] = jnp.dot(yf[:, :rows], zrow[pl.ds(0, rows), :], preferred_element_type=F32)
-    @pl.when(is_late(g))
-    def _():
-        meet()
-
-    for copy in swap:
-        copy.wait_recv()
+    waiter(mag.at[1], pair_sem.at[0], swap_recv.at[0]).wait_recv()
     for comp in range(3):
         at = pl.ds(2 * comp * half, 2 * half)
         part = spec[:, at] + jnp.dot(yf[:, rows:], along_z(1, comp), preferred_element_type=F32)
@@ -241,16 +250,6 @@
         @pl.when(jnp.logical_not(jnp.logical_and(lower, is_late(to))))
         def _():
             forward(to).start()
-
-    def waiter(ref, send_sem, recv_sem):
-        return pltpu.make_async_remote_copy(
-            src_ref=ref,
-            dst_ref=ref,
-            send_sem=send_sem,
-            recv_sem=recv_sem,
-            device_id=(g, other),
-            device_id_type=MESH,
-        )
 
     lane = lax.broadcasted_iota(jnp.int32, (own, half), 1)
     row = lax.broadcasted_iota(jnp.int32, (own, half), 0)
@@ -400,14 +399,27 @@
             def _():
                 backward(i, 0).start()
 
-        def over(n, carry):
+        def serve(n):
             i = target_back(n)
             spread(i, add_layer(layer, sources, i))
 
+        chunk = 3
+
+        def over(n, carry):
+            first = 1 + n * chunk
+            serve(first)
+
+            @pl.when(n == 0)
+            def _():
+                dispatch(0)
+
             @pl.when(n > 0)
             def _():
-                dispatch(jnp.maximum(n - 1, 0))
-
+                for p in range(chunk):
+                    dispatch(jnp.maximum(first - chunk + p, 1))
+
+            for p in range(1, chunk):
+                serve(first + p)
             return carry
 
         def spread(i, total):
@@ -423,8 +435,10 @@
                 back[i, :, pl.ds(2 * comp * half, half)] = new_re.astype(BF16)
                 back[i, :, pl.ds((2 * comp + 1) * half, half)] = new_im.astype(BF16)
 
-        lax.fori_loop(0, groups, over, 0)
-        dispatch(groups - 1)
+        serve(0)
+        lax.fori_loop(0, (groups - 1) // chunk, over, 0)
+        for p in range(chunk):
+            dispatch(groups - chunk + p)
 
         @pl.when(c == 1)
         def _():
@@ -593,9 +607,9 @@
             pltpu.VMEM((2, groups, own, wide), BF16),
             pltpu.VMEM((y_total, wide), F32),
             pltpu.VMEM((3, rows, z_total), F32),
-            dma((8,)),
+            dma((6,)),
             dma((1,)),
-            dma((3,)),
+            dma((1,)),
             dma((3,)),
             dma((1,)),
             dma((layers,)),

time: 20.5 us -> 20.5 us (level)
  no operation moved by 1% of the time
where the time goes in v6:
time: 20.5 us; the launch traced here: 20.4 us
  Pallas kernels  19.7 us (96%)
  local copies, waits for them, and re-layouts  0.68 us (3%)
    pallas_call x1, Pallas kernels, on_device(): pl.pallas_call(functools.partial(kernel, groups, pairs), out_shape=pltpu....  19.7 us
    unnamed x1, local copies, waits for them, and re-layouts  0.68 us

profile of v6, /device:TPU:0, one launch (start us, length us, event | category | flops | bytes accessed | tf_op | source)
XLA Modules:
  0.0 20.4 jit_solution(405616507569444303)
XLA Ops:
  0.0 19.7 %shard_map.73 = bf16[3,128,256]{2,1,0:T(8,128)(2,1)S(1)} custom-call(bf16[3,128,256]{2,1,0:T(8,128)(2,1)} %bitcast.9, bf16[128,6,16,256]{3,2,1,0:T(8,128)(2,1)} %newell.1, bf16[2,128,256]{2,1,0:T(8,128)(2,1)} %constant.10.clone.y_fwd, bf16[2,128,256]{2,1,0:T(8,128)(2,1)} %constant.11.clone.y_inv, bf16[256,256]{1,0:T(8,128)(2,1)} %constant.12.clone.z_fwd, ...), custom_call_target="tpu_custom_call" | custom-call | tf_op jit(solution)/shard_map/pallas_call | solution.py:587
  19.7 0.7 %copy.10 = bf16[128,3,1,256]{3,0,2,1:T(8,128)(2,1)} copy(bf16[128,3,1,256]{3,0,2,1:T(8,128)(2,1)S(1)} %bitcast.8) | data formatting | bytes 393216

commit v7 on v6

--- a/solution.py
+++ b/solution.py
@@ -510,9 +510,9 @@
 
     @pl.when(c == 1)
     def _():
-        for k in range(layers):
-            n = relay_at(k)
-            for part in (1, 0):
+        for part in (1, 0):
+            for k in range(layers):
+                n = relay_at(k)
                 sem = bwd_recv.at[part * layers + n]
                 if part == 1:
                     @pl.when(n == my_layer)

time: 20.5 us -> 20.5 us (level)
  no operation moved by 1% of the time
where the time goes in v7:
time: 20.5 us; the launch traced here: 20.3 us
  Pallas kernels  19.6 us (96%)
  local copies, waits for them, and re-layouts  0.68 us (3%)
    pallas_call x1, Pallas kernels, on_device(): pl.pallas_call(functools.partial(kernel, groups, pairs), out_shape=pltpu....  19.6 us
    unnamed x1, local copies, waits for them, and re-layouts  0.68 us

profile of v7, /device:TPU:0, one launch (start us, length us, event | category | flops | bytes accessed | tf_op | source)
XLA Modules:
  0.0 20.3 jit_solution(6625541590600998946)
XLA Ops:
  0.0 19.6 %shard_map.73 = bf16[3,128,256]{2,1,0:T(8,128)(2,1)S(1)} custom-call(bf16[3,128,256]{2,1,0:T(8,128)(2,1)} %bitcast.9, bf16[128,6,16,256]{3,2,1,0:T(8,128)(2,1)} %newell.1, bf16[2,128,256]{2,1,0:T(8,128)(2,1)} %constant.10.clone.y_fwd, bf16[2,128,256]{2,1,0:T(8,128)(2,1)} %constant.11.clone.y_inv, bf16[256,256]{1,0:T(8,128)(2,1)} %constant.12.clone.z_fwd, ...), custom_call_target="tpu_custom_call" | custom-call | tf_op jit(solution)/shard_map/pallas_call | solution.py:587
  19.6 0.7 %copy.10 = bf16[128,3,1,256]{3,0,2,1:T(8,128)(2,1)} copy(bf16[128,3,1,256]{3,0,2,1:T(8,128)(2,1)S(1)} %bitcast.8) | data formatting | bytes 393216

commit v8 on v7

--- a/solution.py
+++ b/solution.py
@@ -106,12 +106,12 @@
     ]
     tabs = [
         pltpu.make_async_copy(z_fwd, zf, load_sem.at[1]),
-        pltpu.make_async_copy(y_fwd.at[c], yf, load_sem.at[2]),
+        pltpu.make_async_copy(y_fwd.at[c], yf, load_sem.at[1]),
     ]
     late = [
-        pltpu.make_async_copy(rev, rv, load_sem.at[3]),
-        pltpu.make_async_copy(y_inv.at[c], yi, load_sem.at[4]),
-        pltpu.make_async_copy(z_inv, zi, load_sem.at[5]),
+        pltpu.make_async_copy(rev, rv, load_sem.at[2]),
+        pltpu.make_async_copy(y_inv.at[c], yi, load_sem.at[3]),
+        pltpu.make_async_copy(z_inv, zi, load_sem.at[3]),
     ]
     for copy in loads:
         copy.start()
@@ -120,14 +120,15 @@
     def _():
         pl.semaphore_signal(barrier, inc=1, device_id=(g, 1), device_id_type=MESH)
 
+    for r in range(1, groups):
+        to = lax.rem(g + r, groups)
+
+        @pl.when(jnp.logical_or(jnp.logical_not(is_late(g)), to >= groups // 2))
+        def _():
+            pl.semaphore_signal(barrier, inc=1, device_id=(to, 0), device_id_type=MESH)
+
     for copy in tabs:
         copy.start()
-    for r in range(1, groups):
-        to = lax.rem(g + r, groups)
-
-        @pl.when(jnp.logical_or(jnp.logical_not(is_late(g)), to >= groups // 2))
-        def _():
-            pl.semaphore_signal(barrier, inc=1, device_id=(to, 0), device_id_type=MESH)
 
     def newell_row(part, p):
         t = (2 * g + part) * pairs + p
@@ -209,8 +210,7 @@
     for p in range(pairs):
         far(p, 1).start()
 
-    for copy in tabs:
-        copy.wait()
+    pltpu.make_async_copy(mag.at[0], mag.at[0], load_sem.at[1]).wait()
     def along_z(side, comp):
         return jnp.dot(mag[side, comp], zf[...], preferred_element_type=F32).astype(BF16)
 
@@ -471,8 +471,7 @@
     lax.fori_loop(0, layers - 1, step, 0)
     finish(group_at(layers - 1))
 
-    for copy in late[1:]:
-        copy.wait()
+    pltpu.make_async_copy(mag.at[0], mag.at[0], load_sem.at[3]).wait()
 
     def relay(part, n):
         at = pl.ds(n * plane, plane)
@@ -574,7 +573,7 @@
     rows, _, x_cells, z_total = magnet.shape
     groups = lax.axis_size("gx")
     parts = lax.axis_size("yz")
-    assert x_cells == 1 and parts == 2
+    assert x_cells == 1 and parts == 2 and rows * parts == z_total
     y_total = rows * parts
     pairs = y_total // (groups * parts * 2)
     own = 2 * pairs
@@ -607,7 +606,7 @@
             pltpu.VMEM((2, groups, own, wide), BF16),
             pltpu.VMEM((y_total, wide), F32),
             pltpu.VMEM((3, rows, z_total), F32),
-            dma((6,)),
+            dma((4,)),
             dma((1,)),
             dma((1,)),
             dma((3,)),

time: 20.5 us -> 20.4 us (level)
  no operation moved by 1% of the time
where the time goes in v8:
time: 20.4 us; the launch traced here: 20.3 us
  Pallas kernels  19.6 us (96%)
  local copies, waits for them, and re-layouts  0.68 us (3%)
    pallas_call x1, Pallas kernels, on_device(): pl.pallas_call(functools.partial(kernel, groups, pairs), out_shape=pltpu....  19.6 us
    unnamed x1, local copies, waits for them, and re-layouts  0.68 us

profile of v8, /device:TPU:0, one launch (start us, length us, event | category | flops | bytes accessed | tf_op | source)
XLA Modules:
  0.0 20.3 jit_solution(9222300111886819952)
XLA Ops:
  0.0 19.6 %shard_map.73 = bf16[3,128,256]{2,1,0:T(8,128)(2,1)S(1)} custom-call(bf16[3,128,256]{2,1,0:T(8,128)(2,1)} %bitcast.9, bf16[128,6,16,256]{3,2,1,0:T(8,128)(2,1)} %newell.1, bf16[2,128,256]{2,1,0:T(8,128)(2,1)} %constant.10.clone.y_fwd, bf16[2,128,256]{2,1,0:T(8,128)(2,1)} %constant.11.clone.y_inv, bf16[256,256]{1,0:T(8,128)(2,1)} %constant.12.clone.z_fwd, ...), custom_call_target="tpu_custom_call" | custom-call | tf_op jit(solution)/shard_map/pallas_call | solution.py:586
  19.6 0.7 %copy.10 = bf16[128,3,1,256]{3,0,2,1:T(8,128)(2,1)} copy(bf16[128,3,1,256]{3,0,2,1:T(8,128)(2,1)S(1)} %bitcast.8) | data formatting | bytes 393216
